TPU v7x, 128 devices: a whole 4x4x4 slice. The times are simulated.
128 devices in a mesh: rows: 4 (over y_hi, core), cols: 4 (over z), heads: 8 (over x, y_lo).
Axes of the slice: x: 4, y: 4 (y_hi: 2, y_lo: 2; y = y_hi * 2 + y_lo), z: 4, core: 2. Of those that a mesh axis runs over, the one named last changes fastest.
Arguments:
- tokens: bfloat16 [16384, 1024], P(('rows', 'cols'), 'heads'), may hold values from -8 to 8
- ln_gain: float32 [1024], replicated, may hold values from 0.1 to 1.9
- w_qkv: bfloat16 [3, 1024, 1024], P(None, None, 'heads'), may hold values from -1 to 1
- w_out: bfloat16 [1024, 1024], P('heads'), may hold values from -0.1875 to 0.1875
- out_bias: float32 [1024], P('heads'), may hold values from -3 to 3
Outputs:
- mixed: bfloat16 [16384, 1024], P(('rows', 'cols'), 'heads')
All inputs are finite; a program needn't handle non-finite values.
Results may differ from a plain program's by a relative error of at most 0.0095.
Values may be sent and summed in bfloat16 or wider, within the bound.
No kernel may reach another device: no remote copies, remote signals or barrier semaphores. Data moves between devices by JAX's collectives and lax.ppermute only.
A program may use at most 64 MiB of HBM per device.

v0:
```python
import functools

import jax
import jax.numpy as jnp
from jax import lax
from jax.experimental import pallas as pl
from jax.experimental.pallas import tpu as pltpu
from jax.sharding import PartitionSpec as P


D = 1024
HD = 64
LOG2E = 1.4426950408889634
QSCALE = LOG2E / HD**0.5
CAP = 2.0**60
AXES = ("rows", "cols", "heads")
bf16 = jnp.bfloat16
f32 = jnp.float32


def perm(move):
    pairs = []
    for i in range(128):
        here = dict(x=(i % 8) // 2, yl=i % 2, z=(i // 8) % 4, yh=i // 64, c=(i // 32) % 2)
        to = {**here, **move(here)}
        pairs.append((i, ((to["yh"] * 2 + to["c"]) * 4 + to["z"]) * 8 + to["x"] * 2 + to["yl"]))
    return pairs


Z_UP = perm(lambda d: dict(z=(d["z"] + 1) % 4))
Z_DOWN = perm(lambda d: dict(z=(d["z"] - 1) % 4))
Z_FAR = perm(lambda d: dict(z=(d["z"] + 2) % 4))
YH_SWAP = perm(lambda d: dict(yh=1 - d["yh"]))
YL_SWAP = perm(lambda d: dict(yl=1 - d["yl"]))
CORE_SWAP = perm(lambda d: dict(c=1 - d["c"]))
X_UP = perm(lambda d: dict(x=(d["x"] + 1) % 4))
X_DOWN = perm(lambda d: dict(x=(d["x"] - 1) % 4))
X_FAR = perm(lambda d: dict(x=(d["x"] + 2) % 4))


def send(x, pairs):
    return lax.ppermute(x, AXES, pairs)


def vmem():
    return pl.BlockSpec(memory_space=pltpu.VMEM)


def hbm():
    return pl.BlockSpec(memory_space=pltpu.HBM)


def smem():
    return pl.BlockSpec(memory_space=pltpu.SMEM)


def project_kernel(ids_ref, own_hbm, *refs):
    x_refs = list(refs[:7])
    gain_ref, w_hbm, kv_ref, q_ref, out_ref, own_ref, w_ref, n_ref, sems = refs[7:]
    own_copy = pltpu.make_async_copy(own_hbm, own_ref, sems.at[0])
    w_copy = pltpu.make_async_copy(w_hbm, w_ref, sems.at[1])
    own_copy.start()
    w_copy.start()
    x_refs = [own_ref] + x_refs
    tok = own_ref.shape[0]
    step = 128
    par = ids_ref[8]
    half = tok // 2
    lane = lax.broadcasted_iota(jnp.int32, (step, 128), 1)
    low = lane < HD
    own_copy.wait()

    def norm(t, _):
        rows = pl.ds(pl.multiple_of(t * step, step), step)
        parts = [x_ref[rows, :].astype(f32) for x_ref in x_refs]
        total = parts[0]
        for p in parts[1:]:
            total = total + p
        mean = jnp.sum(total, axis=1, keepdims=True) * (1.0 / D)
        sq = None
        for h in range(8):
            c = parts[h] - mean
            sq = c * c if sq is None else sq + c * c
        var = jnp.sum(sq, axis=1, keepdims=True) * (1.0 / D)
        inv = lax.rsqrt(var + 1e-06)
        for h in range(8):
            gain = gain_ref[ids_ref[h]]
            n_ref[ids_ref[h], rows] = ((parts[h] - mean) * inv * gain).astype(bf16)
        return 0

    lax.fori_loop(0, tok // step, norm, 0, unroll=2)
    w_copy.wait()

    def one(t, _):
        at = [pl.ds(pl.multiple_of(part * half + t * step, step), step) for part in range(2)]
        normed = [jnp.concatenate([n_ref[h, a] for h in range(8)], axis=1) for a in at]
        normed = jnp.concatenate(normed, axis=0)
        qk = jnp.dot(normed, jnp.concatenate([w_ref[0], w_ref[1]], axis=1), preferred_element_type=f32)
        v = jnp.dot(normed, w_ref[2], preferred_element_type=f32)
        k0, k1 = qk[:step, 128:], qk[step:, 128:]
        first = jnp.where(low, k0, pltpu.roll(k1, HD, 1))
        second = jnp.where(low, pltpu.roll(k0, HD, 1), k1)
        rows = pl.ds(pl.multiple_of(t * step, step), step)
        kv_ref[rows, :] = jnp.where(par > 0, second, first).astype(bf16)
        out_ref[rows, :] = jnp.where(par > 0, first, second).astype(bf16)
        for part in range(2):
            own = slice(part * step, (part + 1) * step)
            block = (part * (half // step) + t) * HD
            vt = v[own].T
            vkeep = jnp.where(par > 0, vt[HD:], vt[:HD])
            vgive = jnp.where(par > 0, vt[:HD], vt[HD:])
            to = pl.ds(pl.multiple_of(half + block, HD), HD)
            kv_ref[to, :] = vkeep.astype(bf16)
            out_ref[to, :] = vgive.astype(bf16)
            qt = (qk[own, :128] * QSCALE).T
            qkeep = jnp.where(par > 0, qt[HD:], qt[:HD])
            qgive = jnp.where(par > 0, qt[:HD], qt[HD:])
            q_ref[pl.ds(pl.multiple_of(block, HD), HD), :] = qkeep.astype(bf16)
            out_ref[pl.ds(pl.multiple_of(tok + block, HD), HD), :] = qgive.astype(bf16)
        return 0

    lax.fori_loop(0, half // step, one, 0, unroll=2)


def project(ids, blocks, gain, w):
    tok = blocks[0].shape[0]
    return pl.pallas_call(
        project_kernel,
        out_shape=(
            jax.ShapeDtypeStruct((tok, 128), bf16),
            jax.ShapeDtypeStruct((tok // 2, 128), bf16),
            jax.ShapeDtypeStruct((tok + tok // 2, 128), bf16),
        ),
        in_specs=[smem(), hbm()] + [vmem()] * 8 + [hbm()],
        out_specs=(vmem(), vmem(), vmem()),
        scratch_shapes=[
            pltpu.VMEM((tok, 128), bf16),
            pltpu.VMEM(w.shape, bf16),
            pltpu.VMEM((8, tok, 128), bf16),
            pltpu.SemaphoreType.DMA((2,)),
        ],
        compiler_params=pltpu.CompilerParams(vmem_limit_bytes=12 << 20),
        name="project",
    )(ids, *blocks, gain, w)


def attend_kernel(*refs, npieces, windows, offset, first, outs, bq, bk, unroll, ahead):
    pieces = refs[:npieces]
    qs = refs[npieces : npieces + len(windows)]
    rest = list(refs[npieces + len(windows) :])
    if not first:
        acc_in, m_in = rest[:2]
        rest = rest[2:]
    out_refs = rest[:outs]
    rest = rest[outs:]
    acc_ref, m_ref, kvs, q2, s = rest
    ntiles = kvs.shape[0]
    per_tile = 1024 // bk
    nkb = ntiles * per_tile
    nqb = q2.shape[0]
    base = 0
    for piece in pieces:
        count = piece.shape[0] // 1024

        def load(i, _, piece=piece, base=base):
            for r in range(0, 1024, 256):
                kvs[base + i, r : r + 256] = piece[pl.ds(pl.multiple_of(i * 1024 + r, 256), 256), :]
            return 0

        lax.fori_loop(0, count, load, 0)
        base += count
    per = bq // 128
    zero = jnp.zeros((HD, bq), bf16)
    jb = 0
    for q, (start, count) in zip(qs, windows):
        for j in range(count // HD // per):
            blocks = [q[start + (j * per + b) * HD : start + (j * per + b + 1) * HD, :] for b in range(per)]
            block = jnp.concatenate(blocks, axis=1)
            q2[jb, 0, 0:HD] = block
            q2[jb, 0, HD:] = zero
            q2[jb, 1, 0:HD] = zero
            q2[jb, 1, HD:] = block
            jb += 1

    def scores(j, i):
        tile, sub = i // per_tile, i % per_tile
        k = kvs[tile, pl.ds(pl.multiple_of(sub * (bk // 2), 128), bk // 2)]
        return [jnp.dot(k, q2[j, e], preferred_element_type=f32) for e in range(2)]

    if first:
        for j in range(nqb):
            top = jnp.dot(kvs[0, 0:128], q2[j, 0], preferred_element_type=f32)
            m_ref[j] = jnp.max(top, axis=0, keepdims=True)
    else:
        for j in range(nqb):
            m_ref[j] = m_in[offset + j]

    def reset(j, _):
        acc_ref[j] = jnp.zeros(acc_ref.shape[1:], f32) if first else acc_in[offset + j]
        return 0

    lax.fori_loop(0, nqb, reset, 0)

    steps = nqb * nkb

    units = [(c, g) for c in range(bk // 256) for g in range(bq // 256)]

    def unit(j, i, c, g):
        tile, sub = i // per_tile, i % per_tile
        half, row = (c * 256) // (bk // 2), (c * 256) % (bk // 2)
        k = kvs[tile, pl.ds(pl.multiple_of(sub * (bk // 2) + row, 128), 256)]
        return jnp.dot(k, q2[j, half, :, g * 256 : (g + 1) * 256], preferred_element_type=f32)

    def values(i, c):
        tile, sub = i // per_tile, i % per_tile
        half, row = (c * 256) // (bk // 2), (c * 256) % (bk // 2)
        at = [512 + (half * 4 + sub * (bk // 256) + row // 128 + b) * HD for b in range(2)]
        v = jnp.concatenate([kvs[tile, pl.ds(pl.multiple_of(x, HD), HD)] for x in at], axis=1)
        return jnp.concatenate([v, jnp.ones((16, 256), bf16)], axis=0)

    def trip(t):
        j, i = t // nkb, t % nkb
        u = jnp.where(t + 1 < steps, t + 1, 0)
        todo = [s[n] for n in range(ahead)] if ahead else []
        queue = [(j, i, c, g) for c, g in units]
        later = [(u // nkb, u % nkb, c, g) for c, g in units[:ahead]]
        order = queue[ahead:] + later
        accs = [acc_ref[j, :, g * 256 : (g + 1) * 256] for g in range(bq // 256)]
        tops = [m_ref[j, :, g * 256 : (g + 1) * 256] for g in range(bq // 256)]
        if not ahead:
            todo = [unit(*order.pop(0))]
        made = []
        for n, (jj, ii, c, g) in enumerate(queue):
            if order:
                nxt = unit(*order.pop(0))
                if len(order) < ahead and ahead:
                    made.append(nxt)
                else:
                    todo.append(nxt)
            p = jnp.exp2(todo[n] - tops[g]).astype(bf16)
            accs[g] = accs[g] + jnp.dot(values(i, c), p, preferred_element_type=f32)
        for n, v in enumerate(made):
            s[n] = v
        for g in range(bq // 256):
            acc_ref[j, :, g * 256 : (g + 1) * 256] = accs[g]

    def exact(j, _):
        def widen(i, top):
            for part in scores(j, i):
                top = jnp.maximum(top, jnp.max(part, axis=0, keepdims=True))
            return top

        if first:
            top = lax.fori_loop(0, nkb, widen, jnp.full((1, bq), -jnp.inf, f32))
            acc_ref[j] = jnp.zeros(acc_ref.shape[1:], f32)
        else:
            old = m_in[offset + j]
            top = lax.fori_loop(0, nkb, widen, old)
            acc_ref[j] = acc_in[offset + j] * jnp.exp2(old - top)
        m_ref[j] = top
        return 0

    def sweep(turn):
        @pl.when(turn > 0)
        def _():
            lax.fori_loop(0, nqb, exact, 0)

        for n in range(ahead):
            s[n] = unit(0, 0, *units[n])

        def some(h, _):
            for r in range(unroll):
                trip(unroll * h + r)
            return 0

        lax.fori_loop(0, steps // unroll, some, 0)
        den = acc_ref[:, HD : HD + 1, :]
        fine = jnp.min(jnp.where(den < CAP, 1.0, 0.0)) > 0.5
        return jnp.where(jnp.logical_or(turn > 0, fine), 2, 1)

    lax.while_loop(lambda turn: turn < 2, sweep, 0)

    for n, out_ref in enumerate(out_refs):
        for j in range(nqb // outs):
            a = acc_ref[n * (nqb // outs) + j]
            o = (a[0:HD] * (1.0 / a[HD : HD + 1])).astype(bf16)
            for b in range(per):
                out_ref[(j * per + b) * HD : (j * per + b + 1) * HD, :] = o[:, b * 128 : (b + 1) * 128]


def attend(pieces, qs, state=None, offset=0, outs=0, bq=512, bk=1024, unroll=8, ahead=4):
    windows = tuple(w for q, w in qs)
    nkeys = sum(p.shape[0] for p in pieces)
    nqueries = sum(count for start, count in windows) * 2
    nqb = nqueries // bq
    acc_shape = (nqb, HD + 16, bq)
    m_shape = (nqb, 1, bq)
    scratch = [
        pltpu.VMEM((nkeys // 1024, 1024, 128), bf16),
        pltpu.VMEM((nqb, 2, 128, bq), bf16),
        pltpu.VMEM((max(ahead, 1), 256, 256), f32),
    ]
    if outs:
        out_shape = [jax.ShapeDtypeStruct((nqueries // 2 // outs, 128), bf16)] * outs
        out_specs = [vmem()] * outs
        scratch = [pltpu.VMEM(acc_shape, f32), pltpu.VMEM(m_shape, f32)] + scratch
    else:
        out_shape = (jax.ShapeDtypeStruct(acc_shape, f32), jax.ShapeDtypeStruct(m_shape, f32))
        out_specs = (vmem(), vmem())
    args = [*pieces, *(q for q, w in qs)] + ([] if state is None else list(state))
    flops = 4 * nkeys * nqueries * 128
    return pl.pallas_call(
        functools.partial(
            attend_kernel, npieces=len(pieces), windows=windows, offset=offset, first=state is None, outs=outs, bq=bq, bk=bk, unroll=unroll, ahead=ahead
        ),
        out_shape=out_shape,
        in_specs=[vmem()] * len(args),
        out_specs=out_specs,
        scratch_shapes=scratch,
        compiler_params=pltpu.CompilerParams(vmem_limit_bytes=16 << 20),
        cost_estimate=pl.CostEstimate(flops=flops, transcendentals=nkeys * nqueries, bytes_accessed=nkeys * 256),
    )(*args)


def mix_kernel(pos_ref, *refs, part):
    kept, back, peer_kept, peer_back = refs[:4]
    swap = pos_ref[2] > 0
    own_ref, peer_ref = refs[4:6]
    out_refs = refs[6:10]
    w_ref = refs[10]
    for b in range(4):
        cols = pl.ds(pl.multiple_of((((pos_ref[0] + b) % 4) * 2 + pos_ref[1]) * 128, 128), 128)
        w_ref[0:128, b * 128 : (b + 1) * 128] = own_ref[:, cols]
        w_ref[128:256, b * 128 : (b + 1) * 128] = peer_ref[:, cols]

    count = kept.shape[0] // HD

    def one(t, _):
        at = pl.ds(pl.multiple_of(t * HD, HD), HD)
        also = pl.ds(pl.multiple_of((part * count + t) * HD, HD), HD)
        cols = []
        for mine, other in ((kept, back), (peer_kept, peer_back)):
            a, b = mine[at, :], other[also, :]
            cols += [jnp.where(swap, b, a), jnp.where(swap, a, b)]
        rows = jnp.concatenate(cols, axis=0).T
        out = jnp.dot(rows, w_ref[...], preferred_element_type=f32).astype(bf16)
        to = pl.ds(pl.multiple_of(t * 128, 128), 128)
        for b in range(4):
            out_refs[b][to, :] = out[:, b * 128 : (b + 1) * 128]
        return 0

    lax.fori_loop(0, count, one, 0, unroll=2)


def mix(pos, att, own, peer, part):
    tok = att[0].shape[0] * 2
    return pl.pallas_call(
        functools.partial(mix_kernel, part=part),
        out_shape=[jax.ShapeDtypeStruct((tok, 128), bf16)] * 4,
        in_specs=[smem()] + [vmem()] * 6,
        out_specs=[vmem()] * 4,
        scratch_shapes=[pltpu.VMEM((256, 512), bf16)],
        compiler_params=pltpu.CompilerParams(vmem_limit_bytes=6 << 20),
    )(pos, *att, own, peer)


def per_device(tokens, ln_gain, w_qkv, w_out, out_bias):
    rows = lax.axis_index("rows")
    heads = lax.axis_index("heads")
    yh = rows // 2
    x = heads // 2
    yl = heads % 2
    tok = tokens.shape[0]

    by_y = send(tokens, YL_SWAP)
    by_up = send(tokens, X_UP)
    by_down = send(tokens, X_DOWN)
    y_far = send(by_y, X_FAR)
    y_up = send(by_up, YL_SWAP)
    y_down = send(by_down, YL_SWAP)
    by_far = send(tokens, X_FAR)
    blocks = (tokens, by_up, by_down, by_far, by_y, y_up, y_down, y_far)
    xs = jnp.stack([x, (x + 3) % 4, (x + 1) % 4, (x + 2) % 4])
    ids = jnp.concatenate([xs * 2 + yl, xs * 2 + 1 - yl, yh.reshape(1)]).astype(jnp.int32)

    kv, q, give = project(ids, blocks, ln_gain.reshape(8, 1, 128), pltpu.with_memory_space_constraint(w_qkv, pltpu.HBM))
    got = send(give, YH_SWAP)
    k_other = send(kv, CORE_SWAP)
    k_up = send(kv, Z_UP)
    k_down = send(kv, Z_DOWN)
    kf = got[:tok]
    f_other = send(kf, CORE_SWAP)
    f_up = send(kf, Z_UP)
    f_down = send(kf, Z_DOWN)
    qs = ((got, (tok, tok // 2)), (q, (0, tok // 2)))
    state = attend((kv, kf, k_other, f_other), qs)
    k_up, k_down, f_up, f_down, w_send, state = lax.optimization_barrier((k_up, k_down, f_up, f_down, w_out, state))
    k_far = send(k_up, Z_UP)
    f_far = send(f_down, Z_DOWN)
    ring = (k_up, k_down, f_up, f_down)
    ring = ring + tuple(send(p, CORE_SWAP) for p in ring)
    w_peer = send(w_send, YL_SWAP)
    state = attend(ring, qs, state)
    ends = (k_far, f_far, send(k_far, CORE_SWAP), send(f_far, CORE_SWAP))
    (att_far,) = attend(ends, qs[:1], state, outs=1)
    back = send(att_far, YH_SWAP)
    q_own, att_far = lax.optimization_barrier((q, att_far))
    att = attend(ends, ((q_own, (0, tok // 2)),), state, offset=2, outs=2)
    peer = [send(att[0], YL_SWAP), send(att[1], YL_SWAP)]
    peer_back = send(back, YL_SWAP)
    pos = jnp.stack([x, yl, yh]).astype(jnp.int32)
    parts = []
    for n in range(2):
        part = mix(pos, (att[n], back, peer[n], peer_back), w_out, w_peer, n)
        here = [part[0]]
        for b, pairs in ((1, X_UP), (2, X_FAR), (3, X_DOWN)):
            here.append(send(part[b], pairs))
        parts.append(here)
    summed = sum(jnp.concatenate([parts[0][b], parts[1][b]], axis=0).astype(f32) for b in range(4))
    return (tokens.astype(f32) + summed + out_bias).astype(bf16)


def solution(mesh):
    return jax.shard_map(
        per_device,
        mesh=mesh,
        in_specs=(
            P(("rows", "cols"), "heads"),
            P(),
            P(None, None, "heads"),
            P("heads", None),
            P("heads"),
        ),
        out_specs=P(("rows", "cols"), "heads"),
        check_vma=False,
    )
```

profile of v0, /device:TPU:0, one launch (start us, length us, event | category | flops | bytes accessed | tf_op | source)
XLA Modules:
  0.0 131.4 jit_solution(4486279473343481169)
XLA Ops:
  6.8 2.6 %collective-permute-done.refs_0_ = bf16[1024,128]{1,0:T(8,128)(2,1)S(1)} collective-permute-done((bf16[1024,128]{1,0:T(8,128)(2,1)}, bf16[1024,128]{1,0:T(8,128)(2,1)S(1)}, u32[]{:S(2)}, u32[]{:S(2)}) %collective-permute-start) | collective-permute-done | bytes 262176 | tf_op jit(solution)/shard_map/ppermute | solution.py:42
  9.4 1.9 %collective-permute-start.4 = (bf16[1024,128]{1,0:T(8,128)(2,1)S(1)}, bf16[1024,128]{1,0:T(8,128)(2,1)S(1)}, u32[]{:S(2)}, u32[]{:S(2)}) collective-permute-start(bf16[1024,128]{1,0:T(8,128)(2,1)S(1)} %collective-permute-done.refs_0_), channel_id=1, source_target_pairs={{0,1},{1,0},{2,3},{3,2},{4,5},{5,4},{6,7},{7,6},{8,9},{9,8},{10,11... | collective-permute-start | bytes 786440 | tf_op jit(solution)/shard_map/ppermute | solution.py:42
  11.3 7.7 %collective-permute-start.5 = (bf16[1024,128]{1,0:T(8,128)(2,1)S(1)}, bf16[1024,128]{1,0:T(8,128)(2,1)S(1)}, u32[]{:S(2)}, u32[]{:S(2)}) collective-permute-start(bf16[1024,128]{1,0:T(8,128)(2,1)S(1)} %collective-permute-done.1.refs_1_), channel_id=1, source_target_pairs={{0,1},{1,0},{2,3},{3,2},{4,5},{5,4},{6,7},{7,6},{8,9},{9,8},{10,11... | collective-permute-start | bytes 786440 | tf_op jit(solution)/shard_map/ppermute | solution.py:42
  19.1 4.2 %collective-permute-done.5.refs_5_ = bf16[1024,128]{1,0:T(8,128)(2,1)S(1)} collective-permute-done((bf16[1024,128]{1,0:T(8,128)(2,1)S(1)}, bf16[1024,128]{1,0:T(8,128)(2,1)S(1)}, u32[]{:S(2)}, u32[]{:S(2)}) %collective-permute-start.5) | collective-permute-done | bytes 262176 | tf_op jit(solution)/shard_map/ppermute | solution.py:42
  23.3 3.5 %collective-permute-done.6.refs_6_ = bf16[1024,128]{1,0:T(8,128)(2,1)S(1)} collective-permute-done((bf16[1024,128]{1,0:T(8,128)(2,1)S(1)}, bf16[1024,128]{1,0:T(8,128)(2,1)S(1)}, u32[]{:S(2)}, u32[]{:S(2)}) %collective-permute-start.6) | collective-permute-done | bytes 262176 | tf_op jit(solution)/shard_map/ppermute | solution.py:42
  27.8 3.7 %project.1 = (bf16[1024,128]{1,0:T(8,128)(2,1)S(1)}, bf16[512,128]{1,0:T(8,128)(2,1)S(1)}, bf16[1536,128]{1,0:T(8,128)(2,1)S(1)}) custom-call(s32[9]{0:T(128)S(1)} %pad_add_fusion.1.ids_ref, bf16[1024,128]{1,0:T(8,128)(2,1)S(1)} %copy-done.1, bf16[1024,128]{1,0:T(8,128)(2,1)S(1)} %collective-permute-done.refs_0_, ...), custom_call_target="tpu_custom_call" | custom-call | tf_op jit(solution)/shard_map/project/pallas_call | solution.py:127
  31.6 3.0 %collective-permute-start.9 = (bf16[1536,128]{1,0:T(8,128)(2,1)S(1)}, bf16[1536,128]{1,0:T(8,128)(2,1)S(1)}, u32[]{:S(2)}, u32[]{:S(2)}) collective-permute-start(bf16[1536,128]{1,0:T(8,128)(2,1)S(1)} %get-tuple-element.31), channel_id=1, source_target_pairs={{0,64},{1,65},{2,66},{3,67},{4,68},{5,69},{6,70},{7,71},{8,72},{9,... | collective-permute-start | bytes 1179656 | tf_op jit(solution)/shard_map/ppermute | solution.py:42
  34.5 6.4 %collective-permute-done.9.refs_4_.refs_8_ = bf16[1536,128]{1,0:T(8,128)(2,1)S(1)} collective-permute-done((bf16[1536,128]{1,0:T(8,128)(2,1)S(1)}, bf16[1536,128]{1,0:T(8,128)(2,1)S(1)}, u32[]{:S(2)}, u32[]{:S(2)}) %collective-permute-start.9) | collective-permute-done | bytes 393248 | tf_op jit(solution)/shard_map/ppermute | solution.py:42
  41.0 2.0 %collective-permute-start.7 = (bf16[1024,128]{1,0:T(8,128)(2,1)S(1)}, bf16[1024,128]{1,0:T(8,128)(2,1)S(1)}, u32[]{:S(2)}, u32[]{:S(2)}) collective-permute-start(bf16[1024,128]{1,0:T(8,128)(2,1)S(1)} %get-tuple-element.30.refs_0_), channel_id=1, source_target_pairs={{0,8},{1,9},{2,10},{3,11},{4,12},{5,13},{6,14},{7,15},{8,16},{9,17... | collective-permute-start | bytes 786440 | tf_op jit(solution)/shard_map/ppermute | solution.py:42
  43.0 2.2 %collective-permute-start.8 = (bf16[1024,128]{1,0:T(8,128)(2,1)S(1)}, bf16[1024,128]{1,0:T(8,128)(2,1)S(1)}, u32[]{:S(2)}, u32[]{:S(2)}) collective-permute-start(bf16[1024,128]{1,0:T(8,128)(2,1)S(1)} %get-tuple-element.30.refs_0_), channel_id=1, source_target_pairs={{0,24},{1,25},{2,26},{3,27},{4,28},{5,29},{6,30},{7,31},{8,0},{9,1... | collective-permute-start | bytes 786440 | tf_op jit(solution)/shard_map/ppermute | solution.py:42
  45.2 3.2 %collective-permute-start.11 = (bf16[1024,128]{1,0:T(8,128)(2,1)S(1)}, bf16[1024,128]{1,0:T(8,128)(2,1)S(1)}, u32[]{:S(2)}, u32[]{:S(2)}) collective-permute-start(bf16[1024,128]{1,0:T(8,128)(2,1)S(1)} %slice.4.refs_1_), channel_id=1, source_target_pairs={{0,24},{1,25},{2,26},{3,27},{4,28},{5,29},{6,30},{7,31},{8,0},{9,1... | collective-permute-start | bytes 786440 | tf_op jit(solution)/shard_map/ppermute | solution.py:42
  48.5 20.4 %shard_map.55 = (f32[4,80,512]{2,1,0:T(8,128)S(1)}, f32[4,1,512]{2,1,0:T(1,128)S(1)}) custom-call(bf16[1024,128]{1,0:T(8,128)(2,1)S(1)} %get-tuple-element.30.refs_0_, bf16[1024,128]{1,0:T(8,128)(2,1)S(1)} %slice.4.refs_1_, bf16[1024,128]{1,0:T(8,128)(2,1)S(1)} %collective-permute-done.12.refs_2_, bf16[1024,128]{1,0:T(8,128)(2,1)S(1)} %collective-permute-done.13.refs_3_, ...), custom_call_target="tpu_custom_call" | custom-call | flops 4294967296 | bytes 1048576 | tf_op jit(solution)/shard_map/pallas_call | solution.py:312
  69.5 3.0 %collective-permute-start.15 = (bf16[1024,128]{1,0:T(8,128)(2,1)S(1)}, bf16[1024,128]{1,0:T(8,128)(2,1)S(1)}, u32[]{:S(2)}, u32[]{:S(2)}) collective-permute-start(bf16[1024,128]{1,0:T(8,128)(2,1)S(1)} %collective-permute-done.11.refs_3_), channel_id=1, source_target_pairs={{0,24},{1,25},{2,26},{3,27},{4,28},{5,29},{6,30},{7,31},{8,0},{9,1... | collective-permute-start | bytes 786440 | tf_op jit(solution)/shard_map/ppermute | solution.py:42
  73.0 5.9 %collective-permute-done.14.refs_0_ = bf16[1024,128]{1,0:T(8,128)(2,1)S(1)} collective-permute-done((bf16[1024,128]{1,0:T(8,128)(2,1)S(1)}, bf16[1024,128]{1,0:T(8,128)(2,1)S(1)}, u32[]{:S(2)}, u32[]{:S(2)}) %collective-permute-start.14) | collective-permute-done | bytes 262176 | tf_op jit(solution)/shard_map/ppermute | solution.py:42
  79.4 12.9 %shard_map.56 = (f32[4,80,512]{2,1,0:T(8,128)S(1)}, f32[4,1,512]{2,1,0:T(1,128)S(1)}) custom-call(bf16[1024,128]{1,0:T(8,128)(2,1)S(1)} %collective-permute-done.7.refs_0_, bf16[1024,128]{1,0:T(8,128)(2,1)S(1)} %collective-permute-done.8.refs_1_, bf16[1024,128]{1,0:T(8,128)(2,1)S(1)} %collective-permute-done.10.refs_2_, ...), custom_call_target="tpu_custom_call" | custom-call | flops 8589934592 | bytes 2097152 | tf_op jit(solution)/shard_map/pallas_call | solution.py:312
  92.4 3.5 %shard_map.57 = bf16[512,128]{1,0:T(8,128)(2,1)S(1)} custom-call(bf16[1024,128]{1,0:T(8,128)(2,1)S(1)} %collective-permute-done.14.refs_0_, bf16[1024,128]{1,0:T(8,128)(2,1)S(1)} %collective-permute-done.15.refs_1_, bf16[1024,128]{1,0:T(8,128)(2,1)S(1)} %collective-permute-done.16.refs_2_, bf16[1024,128]{1,0:T(8,128)(2,1)S(1)} %collective-permute-done.17.refs_3_, ...), custom_call_target="tpu_custom_call" | custom-call | flops 2147483648 | bytes 1048576 | tf_op jit(solution)/shard_map/pallas_call | solution.py:312
  95.8 3.0 %collective-permute-start.22 = (bf16[512,128]{1,0:T(8,128)(2,1)S(1)}, bf16[512,128]{1,0:T(8,128)(2,1)S(1)}, u32[]{:S(2)}, u32[]{:S(2)}) collective-permute-start(bf16[512,128]{1,0:T(8,128)(2,1)S(1)} %shard_map.57), channel_id=1, source_target_pairs={{0,64},{1,65},{2,66},{3,67},{4,68},{5,69},{6,70},{7,71},{8,72},{9,... | collective-permute-start | bytes 393224 | tf_op jit(solution)/shard_map/ppermute | solution.py:42
  98.9 4.8 %collective-permute-done.22.refs_1_ = bf16[512,128]{1,0:T(8,128)(2,1)S(1)} collective-permute-done((bf16[512,128]{1,0:T(8,128)(2,1)S(1)}, bf16[512,128]{1,0:T(8,128)(2,1)S(1)}, u32[]{:S(2)}, u32[]{:S(2)}) %collective-permute-start.22) | collective-permute-done | bytes 131104 | tf_op jit(solution)/shard_map/ppermute | solution.py:42
  104.2 3.5 %shard_map.58 = (bf16[256,128]{1,0:T(8,128)(2,1)S(1)}, bf16[256,128]{1,0:T(8,128)(2,1)S(1)}) custom-call(bf16[1024,128]{1,0:T(8,128)(2,1)S(1)} %collective-permute-done.14.refs_0_, bf16[1024,128]{1,0:T(8,128)(2,1)S(1)} %collective-permute-done.15.refs_1_, bf16[1024,128]{1,0:T(8,128)(2,1)S(1)} %collective-permute-done.16.refs_2_, ...), custom_call_target="tpu_custom_call" | custom-call | flops 2147483648 | bytes 1048576 | tf_op jit(solution)/shard_map/pallas_call | solution.py:312
  109.4 2.7 %collective-permute-done.23.refs_2_ = bf16[256,128]{1,0:T(8,128)(2,1)S(1)} collective-permute-done((bf16[256,128]{1,0:T(8,128)(2,1)S(1)}, bf16[256,128]{1,0:T(8,128)(2,1)S(1)}, u32[]{:S(2)}, u32[]{:S(2)}) %collective-permute-start.23) | collective-permute-done | bytes 65568 | tf_op jit(solution)/shard_map/ppermute | solution.py:42
  114.3 1.9 %collective-permute-start.26 = (bf16[256,128]{1,0:T(8,128)(2,1)S(1)}, bf16[256,128]{1,0:T(8,128)(2,1)S(1)}, u32[]{:S(2)}, u32[]{:S(2)}) collective-permute-start(bf16[256,128]{1,0:T(8,128)(2,1)S(1)} %get-tuple-element.47.refs_0_), channel_id=1, source_target_pairs={{0,1},{1,0},{2,3},{3,2},{4,5},{5,4},{6,7},{7,6},{8,9},{9,8},{10,11... | collective-permute-start | bytes 196616 | tf_op jit(solution)/shard_map/ppermute | solution.py:42
  116.2 3.7 %collective-permute-start.29 = (bf16[512,128]{1,0:T(8,128)(2,1)S(1)}, bf16[512,128]{1,0:T(8,128)(2,1)S(1)}, u32[]{:S(2)}, u32[]{:S(2)}) collective-permute-start(bf16[512,128]{1,0:T(8,128)(2,1)S(1)} %get-tuple-element.51), channel_id=1, source_target_pairs={{0,4},{1,5},{2,6},{3,7},{4,0},{5,1},{6,2},{7,3},{8,12},{9,13},{10,... | collective-permute-start | bytes 393224 | tf_op jit(solution)/shard_map/ppermute | solution.py:42
  121.0 2.1 %collective-permute-start.28 = (bf16[512,128]{1,0:T(8,128)(2,1)S(1)}, bf16[512,128]{1,0:T(8,128)(2,1)S(1)}, u32[]{:S(2)}, u32[]{:S(2)}) collective-permute-start(bf16[512,128]{1,0:T(8,128)(2,1)S(1)} %get-tuple-element.50), channel_id=1, source_target_pairs={{0,2},{1,3},{2,4},{3,5},{4,6},{5,7},{6,0},{7,1},{8,10},{9,11},{10,... | collective-permute-start | bytes 393224 | tf_op jit(solution)/shard_map/ppermute | solution.py:42
  124.0 2.5 %collective-permute-start.32 = (bf16[512,128]{1,0:T(8,128)(2,1)S(1)}, bf16[512,128]{1,0:T(8,128)(2,1)S(1)}, u32[]{:S(2)}, u32[]{:S(2)}) collective-permute-start(bf16[512,128]{1,0:T(8,128)(2,1)S(1)} %get-tuple-element.54), channel_id=1, source_target_pairs={{0,6},{1,7},{2,0},{3,1},{4,2},{5,3},{6,4},{7,5},{8,14},{9,15},{10,... | collective-permute-start | bytes 393224 | tf_op jit(solution)/shard_map/ppermute | solution.py:42
  (65 shorter events, 21.0 us)
Async XLA Ops:
  0.0 9.4 %collective-permute-start = (bf16[1024,128]{1,0:T(8,128)(2,1)}, bf16[1024,128]{1,0:T(8,128)(2,1)S(1)}, u32[]{:S(2)}, u32[]{:S(2)}) collective-permute-start(bf16[1024,128]{1,0:T(8,128)(2,1)} %own_hbm.1), channel_id=1, source_target_pairs={{0,2},{1,3},{2,4},{3,5},{4,6},{5,7},{6,0},{7,1},{8,10},{9,11},{10,... | collective-permute-start | bytes 786440 | tf_op jit(solution)/shard_map/ppermute | solution.py:42
  1.6 9.7 %collective-permute-start.1 = (bf16[1024,128]{1,0:T(8,128)(2,1)}, bf16[1024,128]{1,0:T(8,128)(2,1)S(1)}, u32[]{:S(2)}, u32[]{:S(2)}) collective-permute-start(bf16[1024,128]{1,0:T(8,128)(2,1)} %own_hbm.1), channel_id=1, source_target_pairs={{0,6},{1,7},{2,0},{3,1},{4,2},{5,3},{6,4},{7,5},{8,14},{9,15},{10,... | collective-permute-start | bytes 786440 | tf_op jit(solution)/shard_map/ppermute | solution.py:42
  3.2 15.8 %collective-permute-start.3 = (bf16[1024,128]{1,0:T(8,128)(2,1)}, bf16[1024,128]{1,0:T(8,128)(2,1)S(1)}, u32[]{:S(2)}, u32[]{:S(2)}) collective-permute-start(bf16[1024,128]{1,0:T(8,128)(2,1)} %own_hbm.1), channel_id=1, source_target_pairs={{0,1},{1,0},{2,3},{3,2},{4,5},{5,4},{6,7},{7,6},{8,9},{9,8},{10,11... | collective-permute-start | bytes 786440 | tf_op jit(solution)/shard_map/ppermute | solution.py:42
  4.9 14.2 %collective-permute-start.2 = (bf16[1024,128]{1,0:T(8,128)(2,1)}, bf16[1024,128]{1,0:T(8,128)(2,1)S(1)}, u32[]{:S(2)}, u32[]{:S(2)}) collective-permute-start(bf16[1024,128]{1,0:T(8,128)(2,1)} %own_hbm.1), channel_id=1, source_target_pairs={{0,4},{1,5},{2,6},{3,7},{4,0},{5,1},{6,2},{7,3},{8,12},{9,13},{10,... | collective-permute-start | bytes 786440 | tf_op jit(solution)/shard_map/ppermute | solution.py:42
  9.4 9.7 %collective-permute-start.4 = (bf16[1024,128]{1,0:T(8,128)(2,1)S(1)}, bf16[1024,128]{1,0:T(8,128)(2,1)S(1)}, u32[]{:S(2)}, u32[]{:S(2)}) collective-permute-start(bf16[1024,128]{1,0:T(8,128)(2,1)S(1)} %collective-permute-done.refs_0_), channel_id=1, source_target_pairs={{0,1},{1,0},{2,3},{3,2},{4,5},{5,4},{6,7},{7,6},{8,9},{9,8},{10,11... | collective-permute-start | bytes 786440 | tf_op jit(solution)/shard_map/ppermute | solution.py:42
  11.3 12.0 %collective-permute-start.5 = (bf16[1024,128]{1,0:T(8,128)(2,1)S(1)}, bf16[1024,128]{1,0:T(8,128)(2,1)S(1)}, u32[]{:S(2)}, u32[]{:S(2)}) collective-permute-start(bf16[1024,128]{1,0:T(8,128)(2,1)S(1)} %collective-permute-done.1.refs_1_), channel_id=1, source_target_pairs={{0,1},{1,0},{2,3},{3,2},{4,5},{5,4},{6,7},{7,6},{8,9},{9,8},{10,11... | collective-permute-start | bytes 786440 | tf_op jit(solution)/shard_map/ppermute | solution.py:42
  19.0 7.9 %collective-permute-start.6 = (bf16[1024,128]{1,0:T(8,128)(2,1)S(1)}, bf16[1024,128]{1,0:T(8,128)(2,1)S(1)}, u32[]{:S(2)}, u32[]{:S(2)}) collective-permute-start(bf16[1024,128]{1,0:T(8,128)(2,1)S(1)} %collective-permute-done.3.refs_3_), channel_id=1, source_target_pairs={{0,4},{1,5},{2,6},{3,7},{4,0},{5,1},{6,2},{7,3},{8,12},{9,13},{10,... | collective-permute-start | bytes 786440 | tf_op jit(solution)/shard_map/ppermute | solution.py:42
  31.6 9.4 %collective-permute-start.9 = (bf16[1536,128]{1,0:T(8,128)(2,1)S(1)}, bf16[1536,128]{1,0:T(8,128)(2,1)S(1)}, u32[]{:S(2)}, u32[]{:S(2)}) collective-permute-start(bf16[1536,128]{1,0:T(8,128)(2,1)S(1)} %get-tuple-element.31), channel_id=1, source_target_pairs={{0,64},{1,65},{2,66},{3,67},{4,68},{5,69},{6,70},{7,71},{8,72},{9,... | collective-permute-start | bytes 1179656 | tf_op jit(solution)/shard_map/ppermute | solution.py:42
  34.5 10.7 %collective-permute-start.12 = (bf16[1024,128]{1,0:T(8,128)(2,1)S(1)}, bf16[1024,128]{1,0:T(8,128)(2,1)S(1)}, u32[]{:S(2)}, u32[]{:S(2)}) collective-permute-start(bf16[1024,128]{1,0:T(8,128)(2,1)S(1)} %get-tuple-element.30.refs_0_), channel_id=1, source_target_pairs={{0,32},{1,33},{2,34},{3,35},{4,36},{5,37},{6,38},{7,39},{8,40},{9,... | collective-permute-start | bytes 786440 | tf_op jit(solution)/shard_map/ppermute | solution.py:42
  40.9 7.5 %collective-permute-start.13 = (bf16[1024,128]{1,0:T(8,128)(2,1)S(1)}, bf16[1024,128]{1,0:T(8,128)(2,1)S(1)}, u32[]{:S(2)}, u32[]{:S(2)}) collective-permute-start(bf16[1024,128]{1,0:T(8,128)(2,1)S(1)} %slice.4.refs_1_), channel_id=1, source_target_pairs={{0,32},{1,33},{2,34},{3,35},{4,36},{5,37},{6,38},{7,39},{8,40},{9,... | collective-permute-start | bytes 786440 | tf_op jit(solution)/shard_map/ppermute | solution.py:42
  41.0 27.8 %collective-permute-start.7 = (bf16[1024,128]{1,0:T(8,128)(2,1)S(1)}, bf16[1024,128]{1,0:T(8,128)(2,1)S(1)}, u32[]{:S(2)}, u32[]{:S(2)}) collective-permute-start(bf16[1024,128]{1,0:T(8,128)(2,1)S(1)} %get-tuple-element.30.refs_0_), channel_id=1, source_target_pairs={{0,8},{1,9},{2,10},{3,11},{4,12},{5,13},{6,14},{7,15},{8,16},{9,17... | collective-permute-start | bytes 786440 | tf_op jit(solution)/shard_map/ppermute | solution.py:42
  43.0 25.8 %collective-permute-start.8 = (bf16[1024,128]{1,0:T(8,128)(2,1)S(1)}, bf16[1024,128]{1,0:T(8,128)(2,1)S(1)}, u32[]{:S(2)}, u32[]{:S(2)}) collective-permute-start(bf16[1024,128]{1,0:T(8,128)(2,1)S(1)} %get-tuple-element.30.refs_0_), channel_id=1, source_target_pairs={{0,24},{1,25},{2,26},{3,27},{4,28},{5,29},{6,30},{7,31},{8,0},{9,1... | collective-permute-start | bytes 786440 | tf_op jit(solution)/shard_map/ppermute | solution.py:42
  45.2 23.7 %collective-permute-start.10 = (bf16[1024,128]{1,0:T(8,128)(2,1)S(1)}, bf16[1024,128]{1,0:T(8,128)(2,1)S(1)}, u32[]{:S(2)}, u32[]{:S(2)}) collective-permute-start(bf16[1024,128]{1,0:T(8,128)(2,1)S(1)} %slice.4.refs_1_), channel_id=1, source_target_pairs={{0,8},{1,9},{2,10},{3,11},{4,12},{5,13},{6,14},{7,15},{8,16},{9,17... | collective-permute-start | bytes 786440 | tf_op jit(solution)/shard_map/ppermute | solution.py:42
  45.2 23.7 %collective-permute-start.11 = (bf16[1024,128]{1,0:T(8,128)(2,1)S(1)}, bf16[1024,128]{1,0:T(8,128)(2,1)S(1)}, u32[]{:S(2)}, u32[]{:S(2)}) collective-permute-start(bf16[1024,128]{1,0:T(8,128)(2,1)S(1)} %slice.4.refs_1_), channel_id=1, source_target_pairs={{0,24},{1,25},{2,26},{3,27},{4,28},{5,29},{6,30},{7,31},{8,0},{9,1... | collective-permute-start | bytes 786440 | tf_op jit(solution)/shard_map/ppermute | solution.py:42
  69.0 9.9 %collective-permute-start.14 = (bf16[1024,128]{1,0:T(8,128)(2,1)S(1)}, bf16[1024,128]{1,0:T(8,128)(2,1)S(1)}, u32[]{:S(2)}, u32[]{:S(2)}) collective-permute-start(bf16[1024,128]{1,0:T(8,128)(2,1)S(1)} %collective-permute-done.7.refs_0_), channel_id=1, source_target_pairs={{0,8},{1,9},{2,10},{3,11},{4,12},{5,13},{6,14},{7,15},{8,16},{9,17... | collective-permute-start | bytes 786440 | tf_op jit(solution)/shard_map/ppermute | solution.py:42
  69.1 10.4 %collective-permute-start.19 = (bf16[1024,128]{1,0:T(8,128)(2,1)S(1)}, bf16[1024,128]{1,0:T(8,128)(2,1)S(1)}, u32[]{:S(2)}, u32[]{:S(2)}) collective-permute-start(bf16[1024,128]{1,0:T(8,128)(2,1)S(1)} %collective-permute-done.8.refs_1_), channel_id=1, source_target_pairs={{0,32},{1,33},{2,34},{3,35},{4,36},{5,37},{6,38},{7,39},{8,40},{9,... | collective-permute-start | bytes 786440 | tf_op jit(solution)/shard_map/ppermute | solution.py:42
  69.5 9.4 %collective-permute-start.15 = (bf16[1024,128]{1,0:T(8,128)(2,1)S(1)}, bf16[1024,128]{1,0:T(8,128)(2,1)S(1)}, u32[]{:S(2)}, u32[]{:S(2)}) collective-permute-start(bf16[1024,128]{1,0:T(8,128)(2,1)S(1)} %collective-permute-done.11.refs_3_), channel_id=1, source_target_pairs={{0,24},{1,25},{2,26},{3,27},{4,28},{5,29},{6,30},{7,31},{8,0},{9,1... | collective-permute-start | bytes 786440 | tf_op jit(solution)/shard_map/ppermute | solution.py:42
  78.9 13.4 %collective-permute-start.16 = (bf16[1024,128]{1,0:T(8,128)(2,1)S(1)}, bf16[1024,128]{1,0:T(8,128)(2,1)S(1)}, u32[]{:S(2)}, u32[]{:S(2)}) collective-permute-start(bf16[1024,128]{1,0:T(8,128)(2,1)S(1)} %collective-permute-done.14.refs_0_), channel_id=1, source_target_pairs={{0,32},{1,33},{2,34},{3,35},{4,36},{5,37},{6,38},{7,39},{8,40},{9,... | collective-permute-start | bytes 786440 | tf_op jit(solution)/shard_map/ppermute | solution.py:42
  78.9 13.4 %collective-permute-start.17 = (bf16[1024,128]{1,0:T(8,128)(2,1)S(1)}, bf16[1024,128]{1,0:T(8,128)(2,1)S(1)}, u32[]{:S(2)}, u32[]{:S(2)}) collective-permute-start(bf16[1024,128]{1,0:T(8,128)(2,1)S(1)} %collective-permute-done.15.refs_1_), channel_id=1, source_target_pairs={{0,32},{1,33},{2,34},{3,35},{4,36},{5,37},{6,38},{7,39},{8,40},{9,... | collective-permute-start | bytes 786440 | tf_op jit(solution)/shard_map/ppermute | solution.py:42
  95.8 8.0 %collective-permute-start.22 = (bf16[512,128]{1,0:T(8,128)(2,1)S(1)}, bf16[512,128]{1,0:T(8,128)(2,1)S(1)}, u32[]{:S(2)}, u32[]{:S(2)}) collective-permute-start(bf16[512,128]{1,0:T(8,128)(2,1)S(1)} %shard_map.57), channel_id=1, source_target_pairs={{0,64},{1,65},{2,66},{3,67},{4,68},{5,69},{6,70},{7,71},{8,72},{9,... | collective-permute-start | bytes 393224 | tf_op jit(solution)/shard_map/ppermute | solution.py:42
  98.8 10.6 %collective-permute-start.25 = (bf16[128,1024]{1,0:T(8,128)(2,1)S(1)}, bf16[128,1024]{1,0:T(8,128)(2,1)S(1)}, u32[]{:S(2)}, u32[]{:S(2)}) collective-permute-start(bf16[128,1024]{1,0:T(8,128)(2,1)S(1)} %copy-done), channel_id=1, source_target_pairs={{0,1},{1,0},{2,3},{3,2},{4,5},{5,4},{6,7},{7,6},{8,9},{9,8},{10,11... | collective-permute-start | bytes 786440 | tf_op jit(solution)/shard_map/ppermute | solution.py:42
  103.8 8.4 %collective-permute-start.24 = (bf16[512,128]{1,0:T(8,128)(2,1)S(1)}, bf16[512,128]{1,0:T(8,128)(2,1)S(1)}, u32[]{:S(2)}, u32[]{:S(2)}) collective-permute-start(bf16[512,128]{1,0:T(8,128)(2,1)S(1)} %collective-permute-done.22.refs_1_), channel_id=1, source_target_pairs={{0,1},{1,0},{2,3},{3,2},{4,5},{5,4},{6,7},{7,6},{8,9},{9,8},{10,11... | collective-permute-start | bytes 393224 | tf_op jit(solution)/shard_map/ppermute | solution.py:42
  113.3 10.6 %collective-permute-start.27 = (bf16[512,128]{1,0:T(8,128)(2,1)S(1)}, bf16[512,128]{1,0:T(8,128)(2,1)S(1)}, u32[]{:S(2)}, u32[]{:S(2)}) collective-permute-start(bf16[512,128]{1,0:T(8,128)(2,1)S(1)} %get-tuple-element.49), channel_id=1, source_target_pairs={{0,2},{1,3},{2,4},{3,5},{4,6},{5,7},{6,0},{7,1},{8,10},{9,11},{10,... | collective-permute-start | bytes 393224 | tf_op jit(solution)/shard_map/ppermute | solution.py:42
  116.2 10.4 %collective-permute-start.29 = (bf16[512,128]{1,0:T(8,128)(2,1)S(1)}, bf16[512,128]{1,0:T(8,128)(2,1)S(1)}, u32[]{:S(2)}, u32[]{:S(2)}) collective-permute-start(bf16[512,128]{1,0:T(8,128)(2,1)S(1)} %get-tuple-element.51), channel_id=1, source_target_pairs={{0,4},{1,5},{2,6},{3,7},{4,0},{5,1},{6,2},{7,3},{8,12},{9,13},{10,... | collective-permute-start | bytes 393224 | tf_op jit(solution)/shard_map/ppermute | solution.py:42
  (14 other events, 79.7 us)
where the time goes:
time: 132 us; the launch traced here: 131 us
  starting transfers between devices  48.6 us (37%)
  Pallas kernels  46.2 us (35%)
  waiting for transfers between devices  33.6 us (25%)
  local copies, waits for them, and re-layouts  1.64 us (1%)
    ppermute x33, starting transfers between devices, send(): return lax.ppermute(x, AXES, pairs)  48.6 us
    pallas_call x4, Pallas kernels, attend(): pl.pallas_call(functools.partial(attend_kernel, npieces=len(pieces), wind...  40.2 us
    ppermute x33, waiting for transfers between devices, send(): return lax.ppermute(x, AXES, pairs)  33.6 us
    pallas_call x1, Pallas kernels, project(): pl.pallas_call(project_kernel, out_shape=(jax.ShapeDtypeStruct((tok, 128)...  3.74 us
  transfers between devices with their start and end apart: 33, of which 10 were waited for; matrix products, arithmetic and copies ran while one was open for 0% of the time, Pallas kernels for 29%

commit v1 on v0

--- a/solution.py
+++ b/solution.py
@@ -54,53 +54,43 @@
     return pl.BlockSpec(memory_space=pltpu.SMEM)
 
 
-def project_kernel(ids_ref, own_hbm, *refs):
-    x_refs = list(refs[:7])
-    gain_ref, w_hbm, kv_ref, q_ref, out_ref, own_ref, w_ref, n_ref, sems = refs[7:]
-    own_copy = pltpu.make_async_copy(own_hbm, own_ref, sems.at[0])
-    w_copy = pltpu.make_async_copy(w_hbm, w_ref, sems.at[1])
-    own_copy.start()
-    w_copy.start()
-    x_refs = [own_ref] + x_refs
-    tok = own_ref.shape[0]
+def project_kernel(ids_ref, *refs):
+    x_refs = refs[:8]
+    gain_ref, w_ref, kv_ref, q_ref, out_ref, n_even, n_odd = refs[8:]
+    tok = x_refs[0].shape[0]
     step = 128
+    half = tok // 2
     par = ids_ref[8]
-    half = tok // 2
     lane = lax.broadcasted_iota(jnp.int32, (step, 128), 1)
     low = lane < HD
-    own_copy.wait()
-
-    def norm(t, _):
-        rows = pl.ds(pl.multiple_of(t * step, step), step)
-        parts = [x_ref[rows, :].astype(f32) for x_ref in x_refs]
-        total = parts[0]
-        for p in parts[1:]:
-            total = total + p
-        mean = jnp.sum(total, axis=1, keepdims=True) * (1.0 / D)
-        sq = None
-        for h in range(8):
-            c = parts[h] - mean
-            sq = c * c if sq is None else sq + c * c
-        var = jnp.sum(sq, axis=1, keepdims=True) * (1.0 / D)
-        inv = lax.rsqrt(var + 1e-06)
-        for h in range(8):
-            gain = gain_ref[ids_ref[h]]
-            n_ref[ids_ref[h], rows] = ((parts[h] - mean) * inv * gain).astype(bf16)
-        return 0
-
-    lax.fori_loop(0, tok // step, norm, 0, unroll=2)
-    w_copy.wait()
-
-    def one(t, _):
-        at = [pl.ds(pl.multiple_of(part * half + t * step, step), step) for part in range(2)]
-        normed = [jnp.concatenate([n_ref[h, a] for h in range(8)], axis=1) for a in at]
-        normed = jnp.concatenate(normed, axis=0)
+
+    def norm(t, n_ref):
+        for part in range(2):
+            for r in range(0, step, 32):
+                rows = slice(part * half + t * step + r, part * half + t * step + r + 32)
+                parts = [x_ref[rows, :].astype(f32) for x_ref in x_refs]
+                total = parts[0]
+                for p in parts[1:]:
+                    total = total + p
+                mean = jnp.sum(total, axis=1, keepdims=True) * (1.0 / D)
+                cs = [p - mean for p in parts]
+                sq = cs[0] * cs[0]
+                for c in cs[1:]:
+                    sq = sq + c * c
+                var = jnp.sum(sq, axis=1, keepdims=True) * (1.0 / D)
+                inv = lax.rsqrt(var + 1e-06)
+                for h in range(8):
+                    to = slice(part * step + r, part * step + r + 32)
+                    n_ref[ids_ref[h], to] = (cs[h] * inv * gain_ref[ids_ref[h]]).astype(bf16)
+
+    def one(t, n_ref):
+        normed = jnp.concatenate([n_ref[h] for h in range(8)], axis=1)
         qk = jnp.dot(normed, jnp.concatenate([w_ref[0], w_ref[1]], axis=1), preferred_element_type=f32)
         v = jnp.dot(normed, w_ref[2], preferred_element_type=f32)
         k0, k1 = qk[:step, 128:], qk[step:, 128:]
         first = jnp.where(low, k0, pltpu.roll(k1, HD, 1))
         second = jnp.where(low, pltpu.roll(k0, HD, 1), k1)
-        rows = pl.ds(pl.multiple_of(t * step, step), step)
+        rows = slice(t * step, (t + 1) * step)
         kv_ref[rows, :] = jnp.where(par > 0, second, first).astype(bf16)
         out_ref[rows, :] = jnp.where(par > 0, first, second).astype(bf16)
         for part in range(2):
@@ -109,17 +99,46 @@
             vt = v[own].T
             vkeep = jnp.where(par > 0, vt[HD:], vt[:HD])
             vgive = jnp.where(par > 0, vt[:HD], vt[HD:])
-            to = pl.ds(pl.multiple_of(half + block, HD), HD)
+            to = slice(half + block, half + block + HD)
             kv_ref[to, :] = vkeep.astype(bf16)
             out_ref[to, :] = vgive.astype(bf16)
             qt = (qk[own, :128] * QSCALE).T
             qkeep = jnp.where(par > 0, qt[HD:], qt[:HD])
             qgive = jnp.where(par > 0, qt[:HD], qt[HD:])
-            q_ref[pl.ds(pl.multiple_of(block, HD), HD), :] = qkeep.astype(bf16)
-            out_ref[pl.ds(pl.multiple_of(tok + block, HD), HD), :] = qgive.astype(bf16)
-        return 0
-
-    lax.fori_loop(0, half // step, one, 0, unroll=2)
+            q_ref[block : block + HD, :] = qkeep.astype(bf16)
+            out_ref[tok + block : tok + block + HD, :] = qgive.astype(bf16)
+
+    bufs = (n_even, n_odd)
+    trips = half // step
+    norm(0, bufs[0])
+    for t in range(trips):
+        if t + 1 < trips:
+            norm(t + 1, bufs[(t + 1) % 2])
+        one(t, bufs[t % 2])
+
+
+def stage_kernel(x_ref, w_ref, xo_ref, wo_ref, sems):
+    copies = [
+        pltpu.make_async_copy(x_ref, xo_ref, sems.at[0]),
+        pltpu.make_async_copy(w_ref, wo_ref, sems.at[1]),
+    ]
+    for c in copies:
+        c.start()
+    for c in copies:
+        c.wait()
+
+
+def stage(x, w):
+    x, w = (pltpu.with_memory_space_constraint(a, pltpu.HBM) for a in (x, w))
+    return pl.pallas_call(
+        stage_kernel,
+        out_shape=(jax.ShapeDtypeStruct(x.shape, x.dtype), jax.ShapeDtypeStruct(w.shape, w.dtype)),
+        in_specs=[hbm(), hbm()],
+        out_specs=(vmem(), vmem()),
+        scratch_shapes=[pltpu.SemaphoreType.DMA((2,))],
+        compiler_params=pltpu.CompilerParams(vmem_limit_bytes=2 << 20),
+        name="stage",
+    )(x, w)
 
 
 def project(ids, blocks, gain, w):
@@ -131,13 +150,11 @@
             jax.ShapeDtypeStruct((tok // 2, 128), bf16),
             jax.ShapeDtypeStruct((tok + tok // 2, 128), bf16),
         ),
-        in_specs=[smem(), hbm()] + [vmem()] * 8 + [hbm()],
+        in_specs=[smem()] + [vmem()] * 10,
         out_specs=(vmem(), vmem(), vmem()),
         scratch_shapes=[
-            pltpu.VMEM((tok, 128), bf16),
-            pltpu.VMEM(w.shape, bf16),
-            pltpu.VMEM((8, tok, 128), bf16),
-            pltpu.SemaphoreType.DMA((2,)),
+            pltpu.VMEM((8, 256, 128), bf16),
+            pltpu.VMEM((8, 256, 128), bf16),
         ],
         compiler_params=pltpu.CompilerParams(vmem_limit_bytes=12 << 20),
         name="project",
@@ -215,8 +232,7 @@
         tile, sub = i // per_tile, i % per_tile
         half, row = (c * 256) // (bk // 2), (c * 256) % (bk // 2)
         at = [512 + (half * 4 + sub * (bk // 256) + row // 128 + b) * HD for b in range(2)]
-        v = jnp.concatenate([kvs[tile, pl.ds(pl.multiple_of(x, HD), HD)] for x in at], axis=1)
-        return jnp.concatenate([v, jnp.ones((16, 256), bf16)], axis=0)
+        return jnp.concatenate([kvs[tile, pl.ds(pl.multiple_of(x, HD), HD)] for x in at], axis=1)
 
     def trip(t):
         j, i = t // nkb, t % nkb
@@ -225,7 +241,8 @@
         queue = [(j, i, c, g) for c, g in units]
         later = [(u // nkb, u % nkb, c, g) for c, g in units[:ahead]]
         order = queue[ahead:] + later
-        accs = [acc_ref[j, :, g * 256 : (g + 1) * 256] for g in range(bq // 256)]
+        accs = [acc_ref[j, :HD, g * 256 : (g + 1) * 256] for g in range(bq // 256)]
+        dens = [acc_ref[j, HD:, g * 256 : (g + 1) * 256] for g in range(bq // 256)]
         tops = [m_ref[j, :, g * 256 : (g + 1) * 256] for g in range(bq // 256)]
         if not ahead:
             todo = [unit(*order.pop(0))]
@@ -237,12 +254,14 @@
                     made.append(nxt)
                 else:
                     todo.append(nxt)
-            p = jnp.exp2(todo[n] - tops[g]).astype(bf16)
-            accs[g] = accs[g] + jnp.dot(values(i, c), p, preferred_element_type=f32)
+            p = jnp.exp2(todo[n] - tops[g])
+            dens[g] = dens[g] + jnp.sum(p.reshape(32, 8, 256), axis=0)
+            accs[g] = accs[g] + jnp.dot(values(i, c), p.astype(bf16), preferred_element_type=f32)
         for n, v in enumerate(made):
             s[n] = v
         for g in range(bq // 256):
-            acc_ref[j, :, g * 256 : (g + 1) * 256] = accs[g]
+            acc_ref[j, :HD, g * 256 : (g + 1) * 256] = accs[g]
+            acc_ref[j, HD:, g * 256 : (g + 1) * 256] = dens[g]
 
     def exact(j, _):
         def widen(i, top):
@@ -274,7 +293,7 @@
             return 0
 
         lax.fori_loop(0, steps // unroll, some, 0)
-        den = acc_ref[:, HD : HD + 1, :]
+        den = acc_ref[:, HD:, :]
         fine = jnp.min(jnp.where(den < CAP, 1.0, 0.0)) > 0.5
         return jnp.where(jnp.logical_or(turn > 0, fine), 2, 1)
 
@@ -283,7 +302,7 @@
     for n, out_ref in enumerate(out_refs):
         for j in range(nqb // outs):
             a = acc_ref[n * (nqb // outs) + j]
-            o = (a[0:HD] * (1.0 / a[HD : HD + 1])).astype(bf16)
+            o = (a[0:HD] * (1.0 / jnp.sum(a[HD:], axis=0, keepdims=True))).astype(bf16)
             for b in range(per):
                 out_ref[(j * per + b) * HD : (j * per + b + 1) * HD, :] = o[:, b * 128 : (b + 1) * 128]
 
@@ -293,7 +312,7 @@
     nkeys = sum(p.shape[0] for p in pieces)
     nqueries = sum(count for start, count in windows) * 2
     nqb = nqueries // bq
-    acc_shape = (nqb, HD + 16, bq)
+    acc_shape = (nqb, HD + 8, bq)
     m_shape = (nqb, 1, bq)
     scratch = [
         pltpu.VMEM((nkeys // 1024, 1024, 128), bf16),
@@ -325,9 +344,10 @@
 def mix_kernel(pos_ref, *refs, part):
     kept, back, peer_kept, peer_back = refs[:4]
     swap = pos_ref[2] > 0
-    own_ref, peer_ref = refs[4:6]
-    out_refs = refs[6:10]
-    w_ref = refs[10]
+    own_ref, peer_ref, x_ref, bias_ref = refs[4:8]
+    base_ref = refs[8]
+    out_refs = refs[9:12]
+    w_ref = refs[12]
     for b in range(4):
         cols = pl.ds(pl.multiple_of((((pos_ref[0] + b) % 4) * 2 + pos_ref[1]) * 128, 128), 128)
         w_ref[0:128, b * 128 : (b + 1) * 128] = own_ref[:, cols]
@@ -343,25 +363,27 @@
             a, b = mine[at, :], other[also, :]
             cols += [jnp.where(swap, b, a), jnp.where(swap, a, b)]
         rows = jnp.concatenate(cols, axis=0).T
-        out = jnp.dot(rows, w_ref[...], preferred_element_type=f32).astype(bf16)
+        out = jnp.dot(rows, w_ref[...], preferred_element_type=f32)
         to = pl.ds(pl.multiple_of(t * 128, 128), 128)
-        for b in range(4):
-            out_refs[b][to, :] = out[:, b * 128 : (b + 1) * 128]
+        come = pl.ds(pl.multiple_of((part * count + t) * 128, 128), 128)
+        base_ref[to, :] = out[:, :128] + x_ref[come, :].astype(f32) + bias_ref[...]
+        for b in range(3):
+            out_refs[b][to, :] = out[:, (b + 1) * 128 : (b + 2) * 128].astype(bf16)
         return 0
 
     lax.fori_loop(0, count, one, 0, unroll=2)
 
 
-def mix(pos, att, own, peer, part):
+def mix(pos, att, own, peer, x, bias, part):
     tok = att[0].shape[0] * 2
     return pl.pallas_call(
         functools.partial(mix_kernel, part=part),
-        out_shape=[jax.ShapeDtypeStruct((tok, 128), bf16)] * 4,
-        in_specs=[smem()] + [vmem()] * 6,
+        out_shape=[jax.ShapeDtypeStruct((tok, 128), f32)] + [jax.ShapeDtypeStruct((tok, 128), bf16)] * 3,
+        in_specs=[smem()] + [vmem()] * 8,
         out_specs=[vmem()] * 4,
         scratch_shapes=[pltpu.VMEM((256, 512), bf16)],
         compiler_params=pltpu.CompilerParams(vmem_limit_bytes=6 << 20),
-    )(pos, *att, own, peer)
+    )(pos, *att, own, peer, x, bias)
 
 
 def per_device(tokens, ln_gain, w_qkv, w_out, out_bias):
@@ -375,15 +397,16 @@
     by_y = send(tokens, YL_SWAP)
     by_up = send(tokens, X_UP)
     by_down = send(tokens, X_DOWN)
+    by_far = send(tokens, X_FAR)
     y_far = send(by_y, X_FAR)
     y_up = send(by_up, YL_SWAP)
     y_down = send(by_down, YL_SWAP)
-    by_far = send(tokens, X_FAR)
-    blocks = (tokens, by_up, by_down, by_far, by_y, y_up, y_down, y_far)
+    held, w_held = stage(tokens, w_qkv)
+    blocks = (held, by_up, by_down, by_far, by_y, y_up, y_down, y_far)
     xs = jnp.stack([x, (x + 3) % 4, (x + 1) % 4, (x + 2) % 4])
     ids = jnp.concatenate([xs * 2 + yl, xs * 2 + 1 - yl, yh.reshape(1)]).astype(jnp.int32)
 
-    kv, q, give = project(ids, blocks, ln_gain.reshape(8, 1, 128), pltpu.with_memory_space_constraint(w_qkv, pltpu.HBM))
+    kv, q, give = project(ids, blocks, ln_gain.reshape(8, 1, 128), w_held)
     got = send(give, YH_SWAP)
     k_other = send(kv, CORE_SWAP)
     k_up = send(kv, Z_UP)
@@ -411,13 +434,13 @@
     pos = jnp.stack([x, yl, yh]).astype(jnp.int32)
     parts = []
     for n in range(2):
-        part = mix(pos, (att[n], back, peer[n], peer_back), w_out, w_peer, n)
+        part = mix(pos, (att[n], back, peer[n], peer_back), w_out, w_peer, tokens, out_bias.reshape(1, 128), n)
         here = [part[0]]
         for b, pairs in ((1, X_UP), (2, X_FAR), (3, X_DOWN)):
             here.append(send(part[b], pairs))
         parts.append(here)
     summed = sum(jnp.concatenate([parts[0][b], parts[1][b]], axis=0).astype(f32) for b in range(4))
-    return (tokens.astype(f32) + summed + out_bias).astype(bf16)
+    return summed.astype(bf16)
 
 
 def solution(mesh):

time: 132 us -> 128 us (0.970)
  local copies, waits for them, and re-layouts: 1.64 us -> 0.04 us
    unnamed x10 -> x8, local copies, waits for them, and re-layouts: 1.62 us -> 0.02 us
    pallas_call x4, Pallas kernels: 40.2 us -> 38.6 us  [attend(): pl.pallas_call(functools.partial(attend_kernel, npieces=len(pieces), wind...]
  transfers between devices with their start and end apart: 33 -> 33, of which waited for: 10 -> 9; matrix products, arithmetic and copies ran while one was open for 0% -> 0% of each run, Pallas kernels for 29% -> 30%
where the time goes in v1:
time: 128 us
  starting transfers between devices  48.6 us (38%)
  Pallas kernels  45.1 us (35%)
  waiting for transfers between devices  32.6 us (25%)
    ppermute x33, starting transfers between devices, send(): return lax.ppermute(x, AXES, pairs)  48.6 us
    pallas_call x4, Pallas kernels, attend(): pl.pallas_call(functools.partial(attend_kernel, npieces=len(pieces), wind...  38.6 us
    ppermute x33, waiting for transfers between devices, send(): return lax.ppermute(x, AXES, pairs)  32.6 us
    pallas_call x1, Pallas kernels, project(): pl.pallas_call(project_kernel, out_shape=(jax.ShapeDtypeStruct((tok, 128)...  3.01 us
  transfers between devices with their start and end apart: 33, of which 9 were waited for; matrix products, arithmetic and copies ran while one was open for 0% of the time, Pallas kernels for 30%

profile of v1, /device:TPU:0, one launch (start us, length us, event | category | flops | bytes accessed | tf_op | source)
XLA Modules:
  0.0 127.7 jit_solution(2135798885551744489)
XLA Ops:
  9.4 1.9 %collective-permute-start.4 = (bf16[1024,128]{1,0:T(8,128)(2,1)S(1)}, bf16[1024,128]{1,0:T(8,128)(2,1)S(1)}, u32[]{:S(2)}, u32[]{:S(2)}) collective-permute-start(bf16[1024,128]{1,0:T(8,128)(2,1)S(1)} %collective-permute-done.refs_1_), channel_id=1, source_target_pairs={{0,1},{1,0},{2,3},{3,2},{4,5},{5,4},{6,7},{7,6},{8,9},{9,8},{10,11... | collective-permute-start | bytes 786440 | tf_op jit(solution)/shard_map/ppermute | solution.py:42
  11.3 7.7 %collective-permute-start.5 = (bf16[1024,128]{1,0:T(8,128)(2,1)S(1)}, bf16[1024,128]{1,0:T(8,128)(2,1)S(1)}, u32[]{:S(2)}, u32[]{:S(2)}) collective-permute-start(bf16[1024,128]{1,0:T(8,128)(2,1)S(1)} %collective-permute-done.1.refs_2_), channel_id=1, source_target_pairs={{0,1},{1,0},{2,3},{3,2},{4,5},{5,4},{6,7},{7,6},{8,9},{9,8},{10,11... | collective-permute-start | bytes 786440 | tf_op jit(solution)/shard_map/ppermute | solution.py:42
  19.1 4.2 %collective-permute-done.5.refs_6_ = bf16[1024,128]{1,0:T(8,128)(2,1)S(1)} collective-permute-done((bf16[1024,128]{1,0:T(8,128)(2,1)S(1)}, bf16[1024,128]{1,0:T(8,128)(2,1)S(1)}, u32[]{:S(2)}, u32[]{:S(2)}) %collective-permute-start.5) | collective-permute-done | bytes 262176 | tf_op jit(solution)/shard_map/ppermute | solution.py:42
  23.3 3.5 %collective-permute-done.6.refs_7_ = bf16[1024,128]{1,0:T(8,128)(2,1)S(1)} collective-permute-done((bf16[1024,128]{1,0:T(8,128)(2,1)S(1)}, bf16[1024,128]{1,0:T(8,128)(2,1)S(1)}, u32[]{:S(2)}, u32[]{:S(2)}) %collective-permute-start.6) | collective-permute-done | bytes 262176 | tf_op jit(solution)/shard_map/ppermute | solution.py:42
  26.9 3.0 %project.1 = (bf16[1024,128]{1,0:T(8,128)(2,1)S(1)}, bf16[512,128]{1,0:T(8,128)(2,1)S(1)}, bf16[1536,128]{1,0:T(8,128)(2,1)S(1)}) custom-call(s32[9]{0:T(128)S(1)} %pad_add_fusion.1.ids_ref, bf16[1024,128]{1,0:T(8,128)(2,1)S(1)} %get-tuple-element.32.refs_0_, bf16[1024,128]{1,0:T(8,128)(2,1)S(1)} %collective-permute-done.refs_1_, ...), custom_call_target="tpu_custom_call" | custom-call | tf_op jit(solution)/shard_map/project/pallas_call | solution.py:146
  29.9 3.0 %collective-permute-start.9 = (bf16[1536,128]{1,0:T(8,128)(2,1)S(1)}, bf16[1536,128]{1,0:T(8,128)(2,1)S(1)}, u32[]{:S(2)}, u32[]{:S(2)}) collective-permute-start(bf16[1536,128]{1,0:T(8,128)(2,1)S(1)} %get-tuple-element.35), channel_id=1, source_target_pairs={{0,64},{1,65},{2,66},{3,67},{4,68},{5,69},{6,70},{7,71},{8,72},{9,... | collective-permute-start | bytes 1179656 | tf_op jit(solution)/shard_map/ppermute | solution.py:42
  32.9 6.4 %collective-permute-done.9.refs_4_.refs_8_ = bf16[1536,128]{1,0:T(8,128)(2,1)S(1)} collective-permute-done((bf16[1536,128]{1,0:T(8,128)(2,1)S(1)}, bf16[1536,128]{1,0:T(8,128)(2,1)S(1)}, u32[]{:S(2)}, u32[]{:S(2)}) %collective-permute-start.9) | collective-permute-done | bytes 393248 | tf_op jit(solution)/shard_map/ppermute | solution.py:42
  39.4 2.0 %collective-permute-start.7 = (bf16[1024,128]{1,0:T(8,128)(2,1)S(1)}, bf16[1024,128]{1,0:T(8,128)(2,1)S(1)}, u32[]{:S(2)}, u32[]{:S(2)}) collective-permute-start(bf16[1024,128]{1,0:T(8,128)(2,1)S(1)} %get-tuple-element.34.refs_0_), channel_id=1, source_target_pairs={{0,8},{1,9},{2,10},{3,11},{4,12},{5,13},{6,14},{7,15},{8,16},{9,17... | collective-permute-start | bytes 786440 | tf_op jit(solution)/shard_map/ppermute | solution.py:42
  41.3 2.2 %collective-permute-start.8 = (bf16[1024,128]{1,0:T(8,128)(2,1)S(1)}, bf16[1024,128]{1,0:T(8,128)(2,1)S(1)}, u32[]{:S(2)}, u32[]{:S(2)}) collective-permute-start(bf16[1024,128]{1,0:T(8,128)(2,1)S(1)} %get-tuple-element.34.refs_0_), channel_id=1, source_target_pairs={{0,24},{1,25},{2,26},{3,27},{4,28},{5,29},{6,30},{7,31},{8,0},{9,1... | collective-permute-start | bytes 786440 | tf_op jit(solution)/shard_map/ppermute | solution.py:42
  43.5 3.2 %collective-permute-start.11 = (bf16[1024,128]{1,0:T(8,128)(2,1)S(1)}, bf16[1024,128]{1,0:T(8,128)(2,1)S(1)}, u32[]{:S(2)}, u32[]{:S(2)}) collective-permute-start(bf16[1024,128]{1,0:T(8,128)(2,1)S(1)} %slice.4.refs_1_), channel_id=1, source_target_pairs={{0,24},{1,25},{2,26},{3,27},{4,28},{5,29},{6,30},{7,31},{8,0},{9,1... | collective-permute-start | bytes 786440 | tf_op jit(solution)/shard_map/ppermute | solution.py:42
  46.8 19.8 %shard_map.55 = (f32[4,72,512]{2,1,0:T(8,128)S(1)}, f32[4,1,512]{2,1,0:T(1,128)S(1)}) custom-call(bf16[1024,128]{1,0:T(8,128)(2,1)S(1)} %get-tuple-element.34.refs_0_, bf16[1024,128]{1,0:T(8,128)(2,1)S(1)} %slice.4.refs_1_, bf16[1024,128]{1,0:T(8,128)(2,1)S(1)} %collective-permute-done.12.refs_2_, bf16[1024,128]{1,0:T(8,128)(2,1)S(1)} %collective-permute-done.13.refs_3_, ...), custom_call_target="tpu_custom_call" | custom-call | flops 4294967296 | bytes 1048576 | tf_op jit(solution)/shard_map/pallas_call | solution.py:331
  67.2 3.0 %collective-permute-start.15 = (bf16[1024,128]{1,0:T(8,128)(2,1)S(1)}, bf16[1024,128]{1,0:T(8,128)(2,1)S(1)}, u32[]{:S(2)}, u32[]{:S(2)}) collective-permute-start(bf16[1024,128]{1,0:T(8,128)(2,1)S(1)} %collective-permute-done.11.refs_3_), channel_id=1, source_target_pairs={{0,24},{1,25},{2,26},{3,27},{4,28},{5,29},{6,30},{7,31},{8,0},{9,1... | collective-permute-start | bytes 786440 | tf_op jit(solution)/shard_map/ppermute | solution.py:42
  70.7 5.9 %collective-permute-done.14.refs_0_ = bf16[1024,128]{1,0:T(8,128)(2,1)S(1)} collective-permute-done((bf16[1024,128]{1,0:T(8,128)(2,1)S(1)}, bf16[1024,128]{1,0:T(8,128)(2,1)S(1)}, u32[]{:S(2)}, u32[]{:S(2)}) %collective-permute-start.14) | collective-permute-done | bytes 262176 | tf_op jit(solution)/shard_map/ppermute | solution.py:42
  77.2 12.3 %shard_map.56 = (f32[4,72,512]{2,1,0:T(8,128)S(1)}, f32[4,1,512]{2,1,0:T(1,128)S(1)}) custom-call(bf16[1024,128]{1,0:T(8,128)(2,1)S(1)} %collective-permute-done.7.refs_0_, bf16[1024,128]{1,0:T(8,128)(2,1)S(1)} %collective-permute-done.8.refs_1_, bf16[1024,128]{1,0:T(8,128)(2,1)S(1)} %collective-permute-done.10.refs_2_, ...), custom_call_target="tpu_custom_call" | custom-call | flops 8589934592 | bytes 2097152 | tf_op jit(solution)/shard_map/pallas_call | solution.py:331
  89.5 3.2 %shard_map.57 = bf16[512,128]{1,0:T(8,128)(2,1)S(1)} custom-call(bf16[1024,128]{1,0:T(8,128)(2,1)S(1)} %collective-permute-done.14.refs_0_, bf16[1024,128]{1,0:T(8,128)(2,1)S(1)} %collective-permute-done.15.refs_1_, bf16[1024,128]{1,0:T(8,128)(2,1)S(1)} %collective-permute-done.16.refs_2_, bf16[1024,128]{1,0:T(8,128)(2,1)S(1)} %collective-permute-done.17.refs_3_, ...), custom_call_target="tpu_custom_call" | custom-call | flops 2147483648 | bytes 1048576 | tf_op jit(solution)/shard_map/pallas_call | solution.py:331
  92.8 3.0 %collective-permute-start.22 = (bf16[512,128]{1,0:T(8,128)(2,1)S(1)}, bf16[512,128]{1,0:T(8,128)(2,1)S(1)}, u32[]{:S(2)}, u32[]{:S(2)}) collective-permute-start(bf16[512,128]{1,0:T(8,128)(2,1)S(1)} %shard_map.57), channel_id=1, source_target_pairs={{0,64},{1,65},{2,66},{3,67},{4,68},{5,69},{6,70},{7,71},{8,72},{9,... | collective-permute-start | bytes 393224 | tf_op jit(solution)/shard_map/ppermute | solution.py:42
  95.9 4.8 %collective-permute-done.22.refs_1_ = bf16[512,128]{1,0:T(8,128)(2,1)S(1)} collective-permute-done((bf16[512,128]{1,0:T(8,128)(2,1)S(1)}, bf16[512,128]{1,0:T(8,128)(2,1)S(1)}, u32[]{:S(2)}, u32[]{:S(2)}) %collective-permute-start.22) | collective-permute-done | bytes 131104 | tf_op jit(solution)/shard_map/ppermute | solution.py:42
  101.2 3.2 %shard_map.58 = (bf16[256,128]{1,0:T(8,128)(2,1)S(1)}, bf16[256,128]{1,0:T(8,128)(2,1)S(1)}) custom-call(bf16[1024,128]{1,0:T(8,128)(2,1)S(1)} %collective-permute-done.14.refs_0_, bf16[1024,128]{1,0:T(8,128)(2,1)S(1)} %collective-permute-done.15.refs_1_, bf16[1024,128]{1,0:T(8,128)(2,1)S(1)} %collective-permute-done.16.refs_2_, ...), custom_call_target="tpu_custom_call" | custom-call | flops 2147483648 | bytes 1048576 | tf_op jit(solution)/shard_map/pallas_call | solution.py:331
  106.2 3.0 %collective-permute-done.23.refs_2_ = bf16[256,128]{1,0:T(8,128)(2,1)S(1)} collective-permute-done((bf16[256,128]{1,0:T(8,128)(2,1)S(1)}, bf16[256,128]{1,0:T(8,128)(2,1)S(1)}, u32[]{:S(2)}, u32[]{:S(2)}) %collective-permute-start.23) | collective-permute-done | bytes 65568 | tf_op jit(solution)/shard_map/ppermute | solution.py:42
  111.2 1.9 %collective-permute-start.26 = (bf16[256,128]{1,0:T(8,128)(2,1)S(1)}, bf16[256,128]{1,0:T(8,128)(2,1)S(1)}, u32[]{:S(2)}, u32[]{:S(2)}) collective-permute-start(bf16[256,128]{1,0:T(8,128)(2,1)S(1)} %get-tuple-element.51.refs_0_), channel_id=1, source_target_pairs={{0,1},{1,0},{2,3},{3,2},{4,5},{5,4},{6,7},{7,6},{8,9},{9,8},{10,11... | collective-permute-start | bytes 196616 | tf_op jit(solution)/shard_map/ppermute | solution.py:42
  113.1 3.5 %collective-permute-start.29 = (bf16[512,128]{1,0:T(8,128)(2,1)S(1)}, bf16[512,128]{1,0:T(8,128)(2,1)S(1)}, u32[]{:S(2)}, u32[]{:S(2)}) collective-permute-start(bf16[512,128]{1,0:T(8,128)(2,1)S(1)} %get-tuple-element.55), channel_id=1, source_target_pairs={{0,4},{1,5},{2,6},{3,7},{4,0},{5,1},{6,2},{7,3},{8,12},{9,13},{10,... | collective-permute-start | bytes 393224 | tf_op jit(solution)/shard_map/ppermute | solution.py:42
  117.7 2.1 %collective-permute-start.28 = (bf16[512,128]{1,0:T(8,128)(2,1)S(1)}, bf16[512,128]{1,0:T(8,128)(2,1)S(1)}, u32[]{:S(2)}, u32[]{:S(2)}) collective-permute-start(bf16[512,128]{1,0:T(8,128)(2,1)S(1)} %get-tuple-element.54), channel_id=1, source_target_pairs={{0,2},{1,3},{2,4},{3,5},{4,6},{5,7},{6,0},{7,1},{8,10},{9,11},{10,... | collective-permute-start | bytes 393224 | tf_op jit(solution)/shard_map/ppermute | solution.py:42
  121.0 2.5 %collective-permute-start.32 = (bf16[512,128]{1,0:T(8,128)(2,1)S(1)}, bf16[512,128]{1,0:T(8,128)(2,1)S(1)}, u32[]{:S(2)}, u32[]{:S(2)}) collective-permute-start(bf16[512,128]{1,0:T(8,128)(2,1)S(1)} %get-tuple-element.58), channel_id=1, source_target_pairs={{0,6},{1,7},{2,0},{3,1},{4,2},{5,3},{6,4},{7,5},{8,14},{9,15},{10,... | collective-permute-start | bytes 393224 | tf_op jit(solution)/shard_map/ppermute | solution.py:42
  123.5 2.9 %collective-permute-done.28 = bf16[512,128]{1,0:T(8,128)(2,1)S(1)} collective-permute-done((bf16[512,128]{1,0:T(8,128)(2,1)S(1)}, bf16[512,128]{1,0:T(8,128)(2,1)S(1)}, u32[]{:S(2)}, u32[]{:S(2)}) %collective-permute-start.28) | collective-permute-done | bytes 131104 | tf_op jit(solution)/shard_map/ppermute | solution.py:42
  (64 shorter events, 19.2 us)
Async XLA Ops:
  0.0 9.4 %collective-permute-start = (bf16[1024,128]{1,0:T(8,128)(2,1)}, bf16[1024,128]{1,0:T(8,128)(2,1)S(1)}, u32[]{:S(2)}, u32[]{:S(2)}) collective-permute-start(bf16[1024,128]{1,0:T(8,128)(2,1)} %refs_6_.3), channel_id=1, source_target_pairs={{0,2},{1,3},{2,4},{3,5},{4,6},{5,7},{6,0},{7,1},{8,10},{9,11},{10,... | collective-permute-start | bytes 786440 | tf_op jit(solution)/shard_map/ppermute | solution.py:42
  1.6 9.7 %collective-permute-start.1 = (bf16[1024,128]{1,0:T(8,128)(2,1)}, bf16[1024,128]{1,0:T(8,128)(2,1)S(1)}, u32[]{:S(2)}, u32[]{:S(2)}) collective-permute-start(bf16[1024,128]{1,0:T(8,128)(2,1)} %refs_6_.3), channel_id=1, source_target_pairs={{0,6},{1,7},{2,0},{3,1},{4,2},{5,3},{6,4},{7,5},{8,14},{9,15},{10,... | collective-permute-start | bytes 786440 | tf_op jit(solution)/shard_map/ppermute | solution.py:42
  3.2 15.8 %collective-permute-start.3 = (bf16[1024,128]{1,0:T(8,128)(2,1)}, bf16[1024,128]{1,0:T(8,128)(2,1)S(1)}, u32[]{:S(2)}, u32[]{:S(2)}) collective-permute-start(bf16[1024,128]{1,0:T(8,128)(2,1)} %refs_6_.3), channel_id=1, source_target_pairs={{0,1},{1,0},{2,3},{3,2},{4,5},{5,4},{6,7},{7,6},{8,9},{9,8},{10,11... | collective-permute-start | bytes 786440 | tf_op jit(solution)/shard_map/ppermute | solution.py:42
  4.9 14.2 %collective-permute-start.2 = (bf16[1024,128]{1,0:T(8,128)(2,1)}, bf16[1024,128]{1,0:T(8,128)(2,1)S(1)}, u32[]{:S(2)}, u32[]{:S(2)}) collective-permute-start(bf16[1024,128]{1,0:T(8,128)(2,1)} %refs_6_.3), channel_id=1, source_target_pairs={{0,4},{1,5},{2,6},{3,7},{4,0},{5,1},{6,2},{7,3},{8,12},{9,13},{10,... | collective-permute-start | bytes 786440 | tf_op jit(solution)/shard_map/ppermute | solution.py:42
  9.4 9.7 %collective-permute-start.4 = (bf16[1024,128]{1,0:T(8,128)(2,1)S(1)}, bf16[1024,128]{1,0:T(8,128)(2,1)S(1)}, u32[]{:S(2)}, u32[]{:S(2)}) collective-permute-start(bf16[1024,128]{1,0:T(8,128)(2,1)S(1)} %collective-permute-done.refs_1_), channel_id=1, source_target_pairs={{0,1},{1,0},{2,3},{3,2},{4,5},{5,4},{6,7},{7,6},{8,9},{9,8},{10,11... | collective-permute-start | bytes 786440 | tf_op jit(solution)/shard_map/ppermute | solution.py:42
  11.3 12.0 %collective-permute-start.5 = (bf16[1024,128]{1,0:T(8,128)(2,1)S(1)}, bf16[1024,128]{1,0:T(8,128)(2,1)S(1)}, u32[]{:S(2)}, u32[]{:S(2)}) collective-permute-start(bf16[1024,128]{1,0:T(8,128)(2,1)S(1)} %collective-permute-done.1.refs_2_), channel_id=1, source_target_pairs={{0,1},{1,0},{2,3},{3,2},{4,5},{5,4},{6,7},{7,6},{8,9},{9,8},{10,11... | collective-permute-start | bytes 786440 | tf_op jit(solution)/shard_map/ppermute | solution.py:42
  19.0 7.9 %collective-permute-start.6 = (bf16[1024,128]{1,0:T(8,128)(2,1)S(1)}, bf16[1024,128]{1,0:T(8,128)(2,1)S(1)}, u32[]{:S(2)}, u32[]{:S(2)}) collective-permute-start(bf16[1024,128]{1,0:T(8,128)(2,1)S(1)} %collective-permute-done.3.refs_4_), channel_id=1, source_target_pairs={{0,4},{1,5},{2,6},{3,7},{4,0},{5,1},{6,2},{7,3},{8,12},{9,13},{10,... | collective-permute-start | bytes 786440 | tf_op jit(solution)/shard_map/ppermute | solution.py:42
  29.9 9.4 %collective-permute-start.9 = (bf16[1536,128]{1,0:T(8,128)(2,1)S(1)}, bf16[1536,128]{1,0:T(8,128)(2,1)S(1)}, u32[]{:S(2)}, u32[]{:S(2)}) collective-permute-start(bf16[1536,128]{1,0:T(8,128)(2,1)S(1)} %get-tuple-element.35), channel_id=1, source_target_pairs={{0,64},{1,65},{2,66},{3,67},{4,68},{5,69},{6,70},{7,71},{8,72},{9,... | collective-permute-start | bytes 1179656 | tf_op jit(solution)/shard_map/ppermute | solution.py:42
  32.9 10.7 %collective-permute-start.12 = (bf16[1024,128]{1,0:T(8,128)(2,1)S(1)}, bf16[1024,128]{1,0:T(8,128)(2,1)S(1)}, u32[]{:S(2)}, u32[]{:S(2)}) collective-permute-start(bf16[1024,128]{1,0:T(8,128)(2,1)S(1)} %get-tuple-element.34.refs_0_), channel_id=1, source_target_pairs={{0,32},{1,33},{2,34},{3,35},{4,36},{5,37},{6,38},{7,39},{8,40},{9,... | collective-permute-start | bytes 786440 | tf_op jit(solution)/shard_map/ppermute | solution.py:42
  39.4 27.2 %collective-permute-start.7 = (bf16[1024,128]{1,0:T(8,128)(2,1)S(1)}, bf16[1024,128]{1,0:T(8,128)(2,1)S(1)}, u32[]{:S(2)}, u32[]{:S(2)}) collective-permute-start(bf16[1024,128]{1,0:T(8,128)(2,1)S(1)} %get-tuple-element.34.refs_0_), channel_id=1, source_target_pairs={{0,8},{1,9},{2,10},{3,11},{4,12},{5,13},{6,14},{7,15},{8,16},{9,17... | collective-permute-start | bytes 786440 | tf_op jit(solution)/shard_map/ppermute | solution.py:42
  41.3 25.3 %collective-permute-start.8 = (bf16[1024,128]{1,0:T(8,128)(2,1)S(1)}, bf16[1024,128]{1,0:T(8,128)(2,1)S(1)}, u32[]{:S(2)}, u32[]{:S(2)}) collective-permute-start(bf16[1024,128]{1,0:T(8,128)(2,1)S(1)} %get-tuple-element.34.refs_0_), channel_id=1, source_target_pairs={{0,24},{1,25},{2,26},{3,27},{4,28},{5,29},{6,30},{7,31},{8,0},{9,1... | collective-permute-start | bytes 786440 | tf_op jit(solution)/shard_map/ppermute | solution.py:42
  43.5 23.1 %collective-permute-start.10 = (bf16[1024,128]{1,0:T(8,128)(2,1)S(1)}, bf16[1024,128]{1,0:T(8,128)(2,1)S(1)}, u32[]{:S(2)}, u32[]{:S(2)}) collective-permute-start(bf16[1024,128]{1,0:T(8,128)(2,1)S(1)} %slice.4.refs_1_), channel_id=1, source_target_pairs={{0,8},{1,9},{2,10},{3,11},{4,12},{5,13},{6,14},{7,15},{8,16},{9,17... | collective-permute-start | bytes 786440 | tf_op jit(solution)/shard_map/ppermute | solution.py:42
  43.5 23.1 %collective-permute-start.11 = (bf16[1024,128]{1,0:T(8,128)(2,1)S(1)}, bf16[1024,128]{1,0:T(8,128)(2,1)S(1)}, u32[]{:S(2)}, u32[]{:S(2)}) collective-permute-start(bf16[1024,128]{1,0:T(8,128)(2,1)S(1)} %slice.4.refs_1_), channel_id=1, source_target_pairs={{0,24},{1,25},{2,26},{3,27},{4,28},{5,29},{6,30},{7,31},{8,0},{9,1... | collective-permute-start | bytes 786440 | tf_op jit(solution)/shard_map/ppermute | solution.py:42
  66.7 9.9 %collective-permute-start.14 = (bf16[1024,128]{1,0:T(8,128)(2,1)S(1)}, bf16[1024,128]{1,0:T(8,128)(2,1)S(1)}, u32[]{:S(2)}, u32[]{:S(2)}) collective-permute-start(bf16[1024,128]{1,0:T(8,128)(2,1)S(1)} %collective-permute-done.7.refs_0_), channel_id=1, source_target_pairs={{0,8},{1,9},{2,10},{3,11},{4,12},{5,13},{6,14},{7,15},{8,16},{9,17... | collective-permute-start | bytes 786440 | tf_op jit(solution)/shard_map/ppermute | solution.py:42
  66.8 10.4 %collective-permute-start.19 = (bf16[1024,128]{1,0:T(8,128)(2,1)S(1)}, bf16[1024,128]{1,0:T(8,128)(2,1)S(1)}, u32[]{:S(2)}, u32[]{:S(2)}) collective-permute-start(bf16[1024,128]{1,0:T(8,128)(2,1)S(1)} %collective-permute-done.8.refs_1_), channel_id=1, source_target_pairs={{0,32},{1,33},{2,34},{3,35},{4,36},{5,37},{6,38},{7,39},{8,40},{9,... | collective-permute-start | bytes 786440 | tf_op jit(solution)/shard_map/ppermute | solution.py:42
  67.2 9.4 %collective-permute-start.15 = (bf16[1024,128]{1,0:T(8,128)(2,1)S(1)}, bf16[1024,128]{1,0:T(8,128)(2,1)S(1)}, u32[]{:S(2)}, u32[]{:S(2)}) collective-permute-start(bf16[1024,128]{1,0:T(8,128)(2,1)S(1)} %collective-permute-done.11.refs_3_), channel_id=1, source_target_pairs={{0,24},{1,25},{2,26},{3,27},{4,28},{5,29},{6,30},{7,31},{8,0},{9,1... | collective-permute-start | bytes 786440 | tf_op jit(solution)/shard_map/ppermute | solution.py:42
  76.6 12.9 %collective-permute-start.16 = (bf16[1024,128]{1,0:T(8,128)(2,1)S(1)}, bf16[1024,128]{1,0:T(8,128)(2,1)S(1)}, u32[]{:S(2)}, u32[]{:S(2)}) collective-permute-start(bf16[1024,128]{1,0:T(8,128)(2,1)S(1)} %collective-permute-done.14.refs_0_), channel_id=1, source_target_pairs={{0,32},{1,33},{2,34},{3,35},{4,36},{5,37},{6,38},{7,39},{8,40},{9,... | collective-permute-start | bytes 786440 | tf_op jit(solution)/shard_map/ppermute | solution.py:42
  76.7 12.9 %collective-permute-start.17 = (bf16[1024,128]{1,0:T(8,128)(2,1)S(1)}, bf16[1024,128]{1,0:T(8,128)(2,1)S(1)}, u32[]{:S(2)}, u32[]{:S(2)}) collective-permute-start(bf16[1024,128]{1,0:T(8,128)(2,1)S(1)} %collective-permute-done.15.refs_1_), channel_id=1, source_target_pairs={{0,32},{1,33},{2,34},{3,35},{4,36},{5,37},{6,38},{7,39},{8,40},{9,... | collective-permute-start | bytes 786440 | tf_op jit(solution)/shard_map/ppermute | solution.py:42
  92.8 8.0 %collective-permute-start.22 = (bf16[512,128]{1,0:T(8,128)(2,1)S(1)}, bf16[512,128]{1,0:T(8,128)(2,1)S(1)}, u32[]{:S(2)}, u32[]{:S(2)}) collective-permute-start(bf16[512,128]{1,0:T(8,128)(2,1)S(1)} %shard_map.57), channel_id=1, source_target_pairs={{0,64},{1,65},{2,66},{3,67},{4,68},{5,69},{6,70},{7,71},{8,72},{9,... | collective-permute-start | bytes 393224 | tf_op jit(solution)/shard_map/ppermute | solution.py:42
  95.8 10.4 %collective-permute-start.25 = (bf16[128,1024]{1,0:T(8,128)(2,1)S(1)}, bf16[128,1024]{1,0:T(8,128)(2,1)S(1)}, u32[]{:S(2)}, u32[]{:S(2)}) collective-permute-start(bf16[128,1024]{1,0:T(8,128)(2,1)S(1)} %copy-done.1), channel_id=1, source_target_pairs={{0,1},{1,0},{2,3},{3,2},{4,5},{5,4},{6,7},{7,6},{8,9},{9,8},{10,11... | collective-permute-start | bytes 786440 | tf_op jit(solution)/shard_map/ppermute | solution.py:42
  100.7 8.4 %collective-permute-start.24 = (bf16[512,128]{1,0:T(8,128)(2,1)S(1)}, bf16[512,128]{1,0:T(8,128)(2,1)S(1)}, u32[]{:S(2)}, u32[]{:S(2)}) collective-permute-start(bf16[512,128]{1,0:T(8,128)(2,1)S(1)} %collective-permute-done.22.refs_1_), channel_id=1, source_target_pairs={{0,1},{1,0},{2,3},{3,2},{4,5},{5,4},{6,7},{7,6},{8,9},{9,8},{10,11... | collective-permute-start | bytes 393224 | tf_op jit(solution)/shard_map/ppermute | solution.py:42
  110.3 10.7 %collective-permute-start.27 = (bf16[512,128]{1,0:T(8,128)(2,1)S(1)}, bf16[512,128]{1,0:T(8,128)(2,1)S(1)}, u32[]{:S(2)}, u32[]{:S(2)}) collective-permute-start(bf16[512,128]{1,0:T(8,128)(2,1)S(1)} %get-tuple-element.53), channel_id=1, source_target_pairs={{0,2},{1,3},{2,4},{3,5},{4,6},{5,7},{6,0},{7,1},{8,10},{9,11},{10,... | collective-permute-start | bytes 393224 | tf_op jit(solution)/shard_map/ppermute | solution.py:42
  113.1 10.4 %collective-permute-start.29 = (bf16[512,128]{1,0:T(8,128)(2,1)S(1)}, bf16[512,128]{1,0:T(8,128)(2,1)S(1)}, u32[]{:S(2)}, u32[]{:S(2)}) collective-permute-start(bf16[512,128]{1,0:T(8,128)(2,1)S(1)} %get-tuple-element.55), channel_id=1, source_target_pairs={{0,4},{1,5},{2,6},{3,7},{4,0},{5,1},{6,2},{7,3},{8,12},{9,13},{10,... | collective-permute-start | bytes 393224 | tf_op jit(solution)/shard_map/ppermute | solution.py:42
  117.7 8.6 %collective-permute-start.28 = (bf16[512,128]{1,0:T(8,128)(2,1)S(1)}, bf16[512,128]{1,0:T(8,128)(2,1)S(1)}, u32[]{:S(2)}, u32[]{:S(2)}) collective-permute-start(bf16[512,128]{1,0:T(8,128)(2,1)S(1)} %get-tuple-element.54), channel_id=1, source_target_pairs={{0,2},{1,3},{2,4},{3,5},{4,6},{5,7},{6,0},{7,1},{8,10},{9,11},{10,... | collective-permute-start | bytes 393224 | tf_op jit(solution)/shard_map/ppermute | solution.py:42
  (13 other events, 87.9 us)

commit v2 on v1

--- a/solution.py
+++ b/solution.py
@@ -29,6 +29,7 @@
 
 Z_UP = perm(lambda d: dict(z=(d["z"] + 1) % 4))
 Z_DOWN = perm(lambda d: dict(z=(d["z"] - 1) % 4))
+Z_BY_CORE = perm(lambda d: dict(z=(d["z"] + 1 - 2 * d["c"]) % 4))
 Z_FAR = perm(lambda d: dict(z=(d["z"] + 2) % 4))
 YH_SWAP = perm(lambda d: dict(yh=1 - d["yh"]))
 YL_SWAP = perm(lambda d: dict(yl=1 - d["yl"]))
@@ -55,8 +56,9 @@
 
 
 def project_kernel(ids_ref, *refs):
-    x_refs = refs[:8]
-    gain_ref, w_ref, kv_ref, q_ref, out_ref, n_even, n_odd = refs[8:]
+    x_refs = refs[:7]
+    halves = refs[7:9]
+    gain_ref, w_ref, kv_ref, q_ref, out_ref, n_even, n_odd = refs[9:]
     tok = x_refs[0].shape[0]
     step = 128
     half = tok // 2
@@ -69,6 +71,7 @@
             for r in range(0, step, 32):
                 rows = slice(part * half + t * step + r, part * half + t * step + r + 32)
                 parts = [x_ref[rows, :].astype(f32) for x_ref in x_refs]
+                parts.append(halves[part][t * step + r : t * step + r + 32, :].astype(f32))
                 total = parts[0]
                 for p in parts[1:]:
                     total = total + p
@@ -150,7 +153,7 @@
             jax.ShapeDtypeStruct((tok // 2, 128), bf16),
             jax.ShapeDtypeStruct((tok + tok // 2, 128), bf16),
         ),
-        in_specs=[smem()] + [vmem()] * 10,
+        in_specs=[smem()] + [vmem()] * 11,
         out_specs=(vmem(), vmem(), vmem()),
         scratch_shapes=[
             pltpu.VMEM((8, 256, 128), bf16),
@@ -341,7 +344,7 @@
     )(*args)
 
 
-def mix_kernel(pos_ref, *refs, part):
+def mix_kernel(pos_ref, *refs):
     kept, back, peer_kept, peer_back = refs[:4]
     swap = pos_ref[2] > 0
     own_ref, peer_ref, x_ref, bias_ref = refs[4:8]
@@ -357,16 +360,14 @@
 
     def one(t, _):
         at = pl.ds(pl.multiple_of(t * HD, HD), HD)
-        also = pl.ds(pl.multiple_of((part * count + t) * HD, HD), HD)
         cols = []
         for mine, other in ((kept, back), (peer_kept, peer_back)):
-            a, b = mine[at, :], other[also, :]
+            a, b = mine[at, :], other[at, :]
             cols += [jnp.where(swap, b, a), jnp.where(swap, a, b)]
         rows = jnp.concatenate(cols, axis=0).T
         out = jnp.dot(rows, w_ref[...], preferred_element_type=f32)
         to = pl.ds(pl.multiple_of(t * 128, 128), 128)
-        come = pl.ds(pl.multiple_of((part * count + t) * 128, 128), 128)
-        base_ref[to, :] = out[:, :128] + x_ref[come, :].astype(f32) + bias_ref[...]
+        base_ref[to, :] = out[:, :128] + x_ref[to, :].astype(f32) + bias_ref[...]
         for b in range(3):
             out_refs[b][to, :] = out[:, (b + 1) * 128 : (b + 2) * 128].astype(bf16)
         return 0
@@ -374,15 +375,16 @@
     lax.fori_loop(0, count, one, 0, unroll=2)
 
 
-def mix(pos, att, own, peer, x, bias, part):
+def mix(pos, att, own, peer, x, bias):
     tok = att[0].shape[0] * 2
     return pl.pallas_call(
-        functools.partial(mix_kernel, part=part),
+        mix_kernel,
         out_shape=[jax.ShapeDtypeStruct((tok, 128), f32)] + [jax.ShapeDtypeStruct((tok, 128), bf16)] * 3,
         in_specs=[smem()] + [vmem()] * 8,
         out_specs=[vmem()] * 4,
         scratch_shapes=[pltpu.VMEM((256, 512), bf16)],
         compiler_params=pltpu.CompilerParams(vmem_limit_bytes=6 << 20),
+        name="mix",
     )(pos, *att, own, peer, x, bias)
 
 
@@ -397,14 +399,15 @@
     by_y = send(tokens, YL_SWAP)
     by_up = send(tokens, X_UP)
     by_down = send(tokens, X_DOWN)
-    by_far = send(tokens, X_FAR)
-    y_far = send(by_y, X_FAR)
     y_up = send(by_up, YL_SWAP)
     y_down = send(by_down, YL_SWAP)
+    y_far = send(by_y, X_FAR)
+    far_lo = send(by_up[: tok // 2], X_UP)
+    far_hi = send(by_down[tok // 2 :], X_DOWN)
     held, w_held = stage(tokens, w_qkv)
-    blocks = (held, by_up, by_down, by_far, by_y, y_up, y_down, y_far)
+    blocks = (held, by_up, by_down, by_y, y_up, y_down, y_far, far_lo, far_hi)
     xs = jnp.stack([x, (x + 3) % 4, (x + 1) % 4, (x + 2) % 4])
-    ids = jnp.concatenate([xs * 2 + yl, xs * 2 + 1 - yl, yh.reshape(1)]).astype(jnp.int32)
+    ids = jnp.concatenate([xs[:3] * 2 + yl, xs * 2 + 1 - yl, xs[3:] * 2 + yl, yh.reshape(1)]).astype(jnp.int32)
 
     kv, q, give = project(ids, blocks, ln_gain.reshape(8, 1, 128), w_held)
     got = send(give, YH_SWAP)
@@ -418,29 +421,25 @@
     qs = ((got, (tok, tok // 2)), (q, (0, tok // 2)))
     state = attend((kv, kf, k_other, f_other), qs)
     k_up, k_down, f_up, f_down, w_send, state = lax.optimization_barrier((k_up, k_down, f_up, f_down, w_out, state))
-    k_far = send(k_up, Z_UP)
-    f_far = send(f_down, Z_DOWN)
+    chosen = jnp.where(rows % 2 > 0, jnp.stack([k_down, f_down]), jnp.stack([k_up, f_up]))
+    far = send(chosen.reshape(2 * tok, 128), Z_BY_CORE)
     ring = (k_up, k_down, f_up, f_down)
     ring = ring + tuple(send(p, CORE_SWAP) for p in ring)
     w_peer = send(w_send, YL_SWAP)
     state = attend(ring, qs, state)
-    ends = (k_far, f_far, send(k_far, CORE_SWAP), send(f_far, CORE_SWAP))
+    ends = (far, send(far, CORE_SWAP))
     (att_far,) = attend(ends, qs[:1], state, outs=1)
     back = send(att_far, YH_SWAP)
     q_own, att_far = lax.optimization_barrier((q, att_far))
-    att = attend(ends, ((q_own, (0, tok // 2)),), state, offset=2, outs=2)
-    peer = [send(att[0], YL_SWAP), send(att[1], YL_SWAP)]
+    (att,) = attend(ends, ((q_own, (0, tok // 2)),), state, offset=2, outs=1)
+    peer = send(att, YL_SWAP)
     peer_back = send(back, YL_SWAP)
     pos = jnp.stack([x, yl, yh]).astype(jnp.int32)
-    parts = []
-    for n in range(2):
-        part = mix(pos, (att[n], back, peer[n], peer_back), w_out, w_peer, tokens, out_bias.reshape(1, 128), n)
-        here = [part[0]]
-        for b, pairs in ((1, X_UP), (2, X_FAR), (3, X_DOWN)):
-            here.append(send(part[b], pairs))
-        parts.append(here)
-    summed = sum(jnp.concatenate([parts[0][b], parts[1][b]], axis=0).astype(f32) for b in range(4))
-    return summed.astype(bf16)
+    parts = mix(pos, (att, back, peer, peer_back), w_out, w_peer, tokens, out_bias.reshape(1, 128))
+    up = send(parts[1], X_UP)
+    across = send(parts[2], X_FAR)
+    down = send(parts[3], X_DOWN)
+    return (parts[0] + up.astype(f32) + across.astype(f32) + down.astype(f32)).astype(bf16)
 
 
 def solution(mesh):

time: 128 us -> 125 us (0.977)
  starting transfers between devices: 48.6 us -> 37.9 us
  waiting for transfers between devices: 32.6 us -> 40.4 us
    ppermute x33 -> x28, starting transfers between devices: 48.6 us -> 37.9 us  [send(): return lax.ppermute(x, AXES, pairs)]
    ppermute x33 -> x28, waiting for transfers between devices: 32.6 us -> 40.4 us  [send(): return lax.ppermute(x, AXES, pairs)]
  transfers between devices with their start and end apart: 33 -> 28, of which waited for: 9 -> 10; matrix products, arithmetic and copies ran while one was open for 0% -> 0% of each run, Pallas kernels for 30% -> 32%
where the time goes in v2:
time: 125 us; the launch traced here: 124 us
  Pallas kernels  44.5 us (36%)
  waiting for transfers between devices  40.4 us (32%)
  starting transfers between devices  37.9 us (30%)
  other arithmetic  1.25 us (1%)
    ppermute x28, waiting for transfers between devices, send(): return lax.ppermute(x, AXES, pairs)  40.4 us
    pallas_call x4, Pallas kernels, attend(): pl.pallas_call(functools.partial(attend_kernel, npieces=len(pieces), wind...  38.6 us
    ppermute x28, starting transfers between devices, send(): return lax.ppermute(x, AXES, pairs)  37.9 us
    pallas_call x1, Pallas kernels, project(): pl.pallas_call(project_kernel, out_shape=(jax.ShapeDtypeStruct((tok, 128)...  3.01 us
  transfers between devices with their start and end apart: 28, of which 10 were waited for; matrix products, arithmetic and copies ran while one was open for 0% of the time, Pallas kernels for 32%

profile of v2, /device:TPU:0, one launch (start us, length us, event | category | flops | bytes accessed | tf_op | source)
XLA Modules:
  0.0 124.3 jit_solution(3746667654616585217)
XLA Ops:
  3.2 1.7 %collective-permute-start.2 = (bf16[1024,128]{1,0:T(8,128)(2,1)}, bf16[1024,128]{1,0:T(8,128)(2,1)S(1)}, u32[]{:S(2)}, u32[]{:S(2)}) collective-permute-start(bf16[1024,128]{1,0:T(8,128)(2,1)} %refs_6_.1), channel_id=1, source_target_pairs={{0,1},{1,0},{2,3},{3,2},{4,5},{5,4},{6,7},{7,6},{8,9},{9,8},{10,11... | collective-permute-start | bytes 786440 | tf_op jit(solution)/shard_map/ppermute | solution.py:43
  4.9 4.5 %collective-permute-done.refs_1_ = bf16[1024,128]{1,0:T(8,128)(2,1)S(1)} collective-permute-done((bf16[1024,128]{1,0:T(8,128)(2,1)}, bf16[1024,128]{1,0:T(8,128)(2,1)S(1)}, u32[]{:S(2)}, u32[]{:S(2)}) %collective-permute-start) | collective-permute-done | bytes 262176 | tf_op jit(solution)/shard_map/ppermute | solution.py:43
  9.4 1.8 %collective-permute-start.3 = (bf16[1024,128]{1,0:T(8,128)(2,1)S(1)}, bf16[1024,128]{1,0:T(8,128)(2,1)S(1)}, u32[]{:S(2)}, u32[]{:S(2)}) collective-permute-start(bf16[1024,128]{1,0:T(8,128)(2,1)S(1)} %collective-permute-done.refs_1_), channel_id=1, source_target_pairs={{0,1},{1,0},{2,3},{3,2},{4,5},{5,4},{6,7},{7,6},{8,9},{9,8},{10,11... | collective-permute-start | bytes 786440 | tf_op jit(solution)/shard_map/ppermute | solution.py:43
  11.4 2.5 %collective-permute-start.5 = (bf16[1024,128]{1,0:T(8,128)(2,1)S(1)}, bf16[1024,128]{1,0:T(8,128)(2,1)S(1)}, u32[]{:S(2)}, u32[]{:S(2)}) collective-permute-start(bf16[1024,128]{1,0:T(8,128)(2,1)S(1)} %collective-permute-done.2.refs_3_), channel_id=1, source_target_pairs={{0,4},{1,5},{2,6},{3,7},{4,0},{5,1},{6,2},{7,3},{8,12},{9,13},{10,... | collective-permute-start | bytes 786440 | tf_op jit(solution)/shard_map/ppermute | solution.py:43
  15.1 2.2 %collective-permute-start.7 = (bf16[512,128]{1,0:T(8,128)(2,1)S(1)}, bf16[512,128]{1,0:T(8,128)(2,1)S(1)}, u32[]{:S(2)}, u32[]{:S(2)}) collective-permute-start(bf16[512,128]{1,0:T(8,128)(2,1)S(1)} %slice.15), channel_id=1, source_target_pairs={{0,6},{1,7},{2,0},{3,1},{4,2},{5,3},{6,4},{7,5},{8,14},{9,15},{10,... | collective-permute-start | bytes 393224 | tf_op jit(solution)/shard_map/ppermute | solution.py:43
  18.8 3.7 %collective-permute-done.6.refs_7_ = bf16[512,128]{1,0:T(8,128)(2,1)S(1)} collective-permute-done((bf16[512,128]{1,0:T(8,128)(2,1)S(1)}, bf16[512,128]{1,0:T(8,128)(2,1)S(1)}, u32[]{:S(2)}, u32[]{:S(2)}) %collective-permute-start.6) | collective-permute-done | bytes 131104 | tf_op jit(solution)/shard_map/ppermute | solution.py:43
  22.5 3.0 %project.1 = (bf16[1024,128]{1,0:T(8,128)(2,1)S(1)}, bf16[512,128]{1,0:T(8,128)(2,1)S(1)}, bf16[1536,128]{1,0:T(8,128)(2,1)S(1)}) custom-call(s32[9]{0:T(128)S(1)} %pad_add_fusion.1.ids_ref, bf16[1024,128]{1,0:T(8,128)(2,1)S(1)} %get-tuple-element.26.refs_0_, bf16[1024,128]{1,0:T(8,128)(2,1)S(1)} %collective-permute-done.refs_1_, ...), custom_call_target="tpu_custom_call" | custom-call | tf_op jit(solution)/shard_map/project/pallas_call | solution.py:149
  25.5 3.4 %collective-permute-start.10 = (bf16[1536,128]{1,0:T(8,128)(2,1)S(1)}, bf16[1536,128]{1,0:T(8,128)(2,1)S(1)}, u32[]{:S(2)}, u32[]{:S(2)}) collective-permute-start(bf16[1536,128]{1,0:T(8,128)(2,1)S(1)} %get-tuple-element.29), channel_id=1, source_target_pairs={{0,64},{1,65},{2,66},{3,67},{4,68},{5,69},{6,70},{7,71},{8,72},{9,... | collective-permute-start | bytes 1179656 | tf_op jit(solution)/shard_map/ppermute | solution.py:43
  28.9 8.7 %collective-permute-done.10.refs_4_.refs_8_.refs_2_ = bf16[1536,128]{1,0:T(8,128)(2,1)S(1)} collective-permute-done((bf16[1536,128]{1,0:T(8,128)(2,1)S(1)}, bf16[1536,128]{1,0:T(8,128)(2,1)S(1)}, u32[]{:S(2)}, u32[]{:S(2)}) %collective-permute-start.10) | collective-permute-done | bytes 393248 | tf_op jit(solution)/shard_map/ppermute | solution.py:43
  37.7 2.0 %collective-permute-start.8 = (bf16[1024,128]{1,0:T(8,128)(2,1)S(1)}, bf16[1024,128]{1,0:T(8,128)(2,1)S(1)}, u32[]{:S(2)}, u32[]{:S(2)}) collective-permute-start(bf16[1024,128]{1,0:T(8,128)(2,1)S(1)} %get-tuple-element.28.refs_0_), channel_id=1, source_target_pairs={{0,8},{1,9},{2,10},{3,11},{4,12},{5,13},{6,14},{7,15},{8,16},{9,17... | collective-permute-start | bytes 786440 | tf_op jit(solution)/shard_map/ppermute | solution.py:43
  39.7 2.2 %collective-permute-start.9 = (bf16[1024,128]{1,0:T(8,128)(2,1)S(1)}, bf16[1024,128]{1,0:T(8,128)(2,1)S(1)}, u32[]{:S(2)}, u32[]{:S(2)}) collective-permute-start(bf16[1024,128]{1,0:T(8,128)(2,1)S(1)} %get-tuple-element.28.refs_0_), channel_id=1, source_target_pairs={{0,24},{1,25},{2,26},{3,27},{4,28},{5,29},{6,30},{7,31},{8,0},{9,1... | collective-permute-start | bytes 786440 | tf_op jit(solution)/shard_map/ppermute | solution.py:43
  41.9 3.2 %collective-permute-start.12 = (bf16[1024,128]{1,0:T(8,128)(2,1)S(1)}, bf16[1024,128]{1,0:T(8,128)(2,1)S(1)}, u32[]{:S(2)}, u32[]{:S(2)}) collective-permute-start(bf16[1024,128]{1,0:T(8,128)(2,1)S(1)} %slice.16.refs_1_), channel_id=1, source_target_pairs={{0,24},{1,25},{2,26},{3,27},{4,28},{5,29},{6,30},{7,31},{8,0},{9,1... | collective-permute-start | bytes 786440 | tf_op jit(solution)/shard_map/ppermute | solution.py:43
  45.2 19.8 %shard_map.55 = (f32[4,72,512]{2,1,0:T(8,128)S(1)}, f32[4,1,512]{2,1,0:T(1,128)S(1)}) custom-call(bf16[1024,128]{1,0:T(8,128)(2,1)S(1)} %get-tuple-element.28.refs_0_, bf16[1024,128]{1,0:T(8,128)(2,1)S(1)} %slice.16.refs_1_, bf16[1024,128]{1,0:T(8,128)(2,1)S(1)} %collective-permute-done.13.refs_2_, bf16[1024,128]{1,0:T(8,128)(2,1)S(1)} %collective-permute-done.14.refs_3_, ...), custom_call_target="tpu_custom_call" | custom-call | flops 4294967296 | bytes 1048576 | tf_op jit(solution)/shard_map/pallas_call | solution.py:334
  67.0 1.7 %collective-permute-start.24 = (bf16[128,1024]{1,0:T(8,128)(2,1)S(1)}, bf16[128,1024]{1,0:T(8,128)(2,1)S(1)}, u32[]{:S(2)}, u32[]{:S(2)}) collective-permute-start(bf16[128,1024]{1,0:T(8,128)(2,1)S(1)} %copy-done.1), channel_id=1, source_target_pairs={{0,1},{1,0},{2,3},{3,2},{4,5},{5,4},{6,7},{7,6},{8,9},{9,8},{10,11... | collective-permute-start | bytes 786440 | tf_op jit(solution)/shard_map/ppermute | solution.py:43
  68.7 7.1 %collective-permute-done.15.refs_0_ = bf16[2048,128]{1,0:T(8,128)(2,1)S(1)} collective-permute-done((bf16[2048,128]{1,0:T(8,128)(2,1)S(1)}, bf16[2048,128]{1,0:T(8,128)(2,1)S(1)}, u32[]{:S(2)}, u32[]{:S(2)}) %collective-permute-start.15) | collective-permute-done | bytes 524320 | tf_op jit(solution)/shard_map/ppermute | solution.py:43
  75.8 12.3 %shard_map.56 = (f32[4,72,512]{2,1,0:T(8,128)S(1)}, f32[4,1,512]{2,1,0:T(1,128)S(1)}) custom-call(bf16[1024,128]{1,0:T(8,128)(2,1)S(1)} %collective-permute-done.8.refs_0_, bf16[1024,128]{1,0:T(8,128)(2,1)S(1)} %collective-permute-done.9.refs_1_, bf16[1024,128]{1,0:T(8,128)(2,1)S(1)} %collective-permute-done.11.refs_2_, ...), custom_call_target="tpu_custom_call" | custom-call | flops 8589934592 | bytes 2097152 | tf_op jit(solution)/shard_map/pallas_call | solution.py:334
  88.1 3.2 %shard_map.57 = bf16[512,128]{1,0:T(8,128)(2,1)S(1)} custom-call(bf16[2048,128]{1,0:T(8,128)(2,1)S(1)} %collective-permute-done.15.refs_0_, bf16[2048,128]{1,0:T(8,128)(2,1)S(1)} %collective-permute-done.16.refs_1_, bf16[1536,128]{1,0:T(8,128)(2,1)S(1)} %collective-permute-done.10.refs_4_.refs_8_.refs_2_, f32[4,72,512]{2,1,0:T(8,128)S(1)} %get-tuple-element.39.refs_3_, ...), custom_call_target="tpu_custom_call" | custom-call | flops 2147483648 | bytes 1048576 | tf_op jit(solution)/shard_map/pallas_call | solution.py:334
  91.4 3.5 %collective-permute-start.21 = (bf16[512,128]{1,0:T(8,128)(2,1)S(1)}, bf16[512,128]{1,0:T(8,128)(2,1)S(1)}, u32[]{:S(2)}, u32[]{:S(2)}) collective-permute-start(bf16[512,128]{1,0:T(8,128)(2,1)S(1)} %shard_map.57), channel_id=1, source_target_pairs={{0,64},{1,65},{2,66},{3,67},{4,68},{5,69},{6,70},{7,71},{8,72},{9,... | collective-permute-start | bytes 393224 | tf_op jit(solution)/shard_map/ppermute | solution.py:43
  94.9 3.2 %shard_map.58.refs_0_ = bf16[512,128]{1,0:T(8,128)(2,1)S(1)} custom-call(bf16[2048,128]{1,0:T(8,128)(2,1)S(1)} %collective-permute-done.15.refs_0_, bf16[2048,128]{1,0:T(8,128)(2,1)S(1)} %collective-permute-done.16.refs_1_, bf16[512,128]{1,0:T(8,128)(2,1)S(1)} %get-tuple-element.41.refs_5_.refs_9_.refs_2_, f32[4,72,512]{2,1,0:T(8,128)S(1)} %get-tuple-element.39.refs_3_, ...), custom_call_target="tpu_custom_call" | custom-call | flops 2147483648 | bytes 1048576 | tf_op jit(solution)/shard_map/pallas_call | solution.py:334
  99.1 1.7 %collective-permute-start.23 = (bf16[512,128]{1,0:T(8,128)(2,1)S(1)}, bf16[512,128]{1,0:T(8,128)(2,1)S(1)}, u32[]{:S(2)}, u32[]{:S(2)}) collective-permute-start(bf16[512,128]{1,0:T(8,128)(2,1)S(1)} %collective-permute-done.21.refs_1_), channel_id=1, source_target_pairs={{0,1},{1,0},{2,3},{3,2},{4,5},{5,4},{6,7},{7,6},{8,9},{9,8},{10,11... | collective-permute-start | bytes 393224 | tf_op jit(solution)/shard_map/ppermute | solution.py:43
  100.9 3.7 %collective-permute-done.22.refs_2_ = bf16[512,128]{1,0:T(8,128)(2,1)S(1)} collective-permute-done((bf16[512,128]{1,0:T(8,128)(2,1)S(1)}, bf16[512,128]{1,0:T(8,128)(2,1)S(1)}, u32[]{:S(2)}, u32[]{:S(2)}) %collective-permute-start.22) | collective-permute-done | bytes 131104 | tf_op jit(solution)/shard_map/ppermute | solution.py:43
  104.6 2.1 %collective-permute-done.23.refs_3_ = bf16[512,128]{1,0:T(8,128)(2,1)S(1)} collective-permute-done((bf16[512,128]{1,0:T(8,128)(2,1)S(1)}, bf16[512,128]{1,0:T(8,128)(2,1)S(1)}, u32[]{:S(2)}, u32[]{:S(2)}) %collective-permute-start.23) | collective-permute-done | bytes 131104 | tf_op jit(solution)/shard_map/ppermute | solution.py:43
  110.9 2.5 %collective-permute-start.27 = (bf16[1024,128]{1,0:T(8,128)(2,1)S(1)}, bf16[1024,128]{1,0:T(8,128)(2,1)S(1)}, u32[]{:S(2)}, u32[]{:S(2)}) collective-permute-start(bf16[1024,128]{1,0:T(8,128)(2,1)S(1)} %get-tuple-element.46), channel_id=1, source_target_pairs={{0,6},{1,7},{2,0},{3,1},{4,2},{5,3},{6,4},{7,5},{8,14},{9,15},{10,... | collective-permute-start | bytes 786440 | tf_op jit(solution)/shard_map/ppermute | solution.py:43
  113.5 9.4 %collective-permute-done.25 = bf16[1024,128]{1,0:T(8,128)(2,1)S(1)} collective-permute-done((bf16[1024,128]{1,0:T(8,128)(2,1)S(1)}, bf16[1024,128]{1,0:T(8,128)(2,1)S(1)}, u32[]{:S(2)}, u32[]{:S(2)}) %collective-permute-start.25) | collective-permute-done | bytes 262176 | tf_op jit(solution)/shard_map/ppermute | solution.py:43
  (56 shorter events, 15.0 us)
Async XLA Ops:
  0.0 9.4 %collective-permute-start = (bf16[1024,128]{1,0:T(8,128)(2,1)}, bf16[1024,128]{1,0:T(8,128)(2,1)S(1)}, u32[]{:S(2)}, u32[]{:S(2)}) collective-permute-start(bf16[1024,128]{1,0:T(8,128)(2,1)} %refs_6_.1), channel_id=1, source_target_pairs={{0,2},{1,3},{2,4},{3,5},{4,6},{5,7},{6,0},{7,1},{8,10},{9,11},{10,... | collective-permute-start | bytes 786440 | tf_op jit(solution)/shard_map/ppermute | solution.py:43
  1.6 9.6 %collective-permute-start.1 = (bf16[1024,128]{1,0:T(8,128)(2,1)}, bf16[1024,128]{1,0:T(8,128)(2,1)S(1)}, u32[]{:S(2)}, u32[]{:S(2)}) collective-permute-start(bf16[1024,128]{1,0:T(8,128)(2,1)} %refs_6_.1), channel_id=1, source_target_pairs={{0,6},{1,7},{2,0},{3,1},{4,2},{5,3},{6,4},{7,5},{8,14},{9,15},{10,... | collective-permute-start | bytes 786440 | tf_op jit(solution)/shard_map/ppermute | solution.py:43
  3.2 8.2 %collective-permute-start.2 = (bf16[1024,128]{1,0:T(8,128)(2,1)}, bf16[1024,128]{1,0:T(8,128)(2,1)S(1)}, u32[]{:S(2)}, u32[]{:S(2)}) collective-permute-start(bf16[1024,128]{1,0:T(8,128)(2,1)} %refs_6_.1), channel_id=1, source_target_pairs={{0,1},{1,0},{2,3},{3,2},{4,5},{5,4},{6,7},{7,6},{8,9},{9,8},{10,11... | collective-permute-start | bytes 786440 | tf_op jit(solution)/shard_map/ppermute | solution.py:43
  9.4 13.1 %collective-permute-start.3 = (bf16[1024,128]{1,0:T(8,128)(2,1)S(1)}, bf16[1024,128]{1,0:T(8,128)(2,1)S(1)}, u32[]{:S(2)}, u32[]{:S(2)}) collective-permute-start(bf16[1024,128]{1,0:T(8,128)(2,1)S(1)} %collective-permute-done.refs_1_), channel_id=1, source_target_pairs={{0,1},{1,0},{2,3},{3,2},{4,5},{5,4},{6,7},{7,6},{8,9},{9,8},{10,11... | collective-permute-start | bytes 786440 | tf_op jit(solution)/shard_map/ppermute | solution.py:43
  11.2 11.3 %collective-permute-start.4 = (bf16[1024,128]{1,0:T(8,128)(2,1)S(1)}, bf16[1024,128]{1,0:T(8,128)(2,1)S(1)}, u32[]{:S(2)}, u32[]{:S(2)}) collective-permute-start(bf16[1024,128]{1,0:T(8,128)(2,1)S(1)} %collective-permute-done.1.refs_2_), channel_id=1, source_target_pairs={{0,1},{1,0},{2,3},{3,2},{4,5},{5,4},{6,7},{7,6},{8,9},{9,8},{10,11... | collective-permute-start | bytes 786440 | tf_op jit(solution)/shard_map/ppermute | solution.py:43
  11.4 11.1 %collective-permute-start.5 = (bf16[1024,128]{1,0:T(8,128)(2,1)S(1)}, bf16[1024,128]{1,0:T(8,128)(2,1)S(1)}, u32[]{:S(2)}, u32[]{:S(2)}) collective-permute-start(bf16[1024,128]{1,0:T(8,128)(2,1)S(1)} %collective-permute-done.2.refs_3_), channel_id=1, source_target_pairs={{0,4},{1,5},{2,6},{3,7},{4,0},{5,1},{6,2},{7,3},{8,12},{9,13},{10,... | collective-permute-start | bytes 786440 | tf_op jit(solution)/shard_map/ppermute | solution.py:43
  14.0 8.5 %collective-permute-start.6 = (bf16[512,128]{1,0:T(8,128)(2,1)S(1)}, bf16[512,128]{1,0:T(8,128)(2,1)S(1)}, u32[]{:S(2)}, u32[]{:S(2)}) collective-permute-start(bf16[512,128]{1,0:T(8,128)(2,1)S(1)} %slice.14), channel_id=1, source_target_pairs={{0,2},{1,3},{2,4},{3,5},{4,6},{5,7},{6,0},{7,1},{8,10},{9,11},{10,... | collective-permute-start | bytes 393224 | tf_op jit(solution)/shard_map/ppermute | solution.py:43
  25.5 12.1 %collective-permute-start.10 = (bf16[1536,128]{1,0:T(8,128)(2,1)S(1)}, bf16[1536,128]{1,0:T(8,128)(2,1)S(1)}, u32[]{:S(2)}, u32[]{:S(2)}) collective-permute-start(bf16[1536,128]{1,0:T(8,128)(2,1)S(1)} %get-tuple-element.29), channel_id=1, source_target_pairs={{0,64},{1,65},{2,66},{3,67},{4,68},{5,69},{6,70},{7,71},{8,72},{9,... | collective-permute-start | bytes 1179656 | tf_op jit(solution)/shard_map/ppermute | solution.py:43
  28.9 13.0 %collective-permute-start.13 = (bf16[1024,128]{1,0:T(8,128)(2,1)S(1)}, bf16[1024,128]{1,0:T(8,128)(2,1)S(1)}, u32[]{:S(2)}, u32[]{:S(2)}) collective-permute-start(bf16[1024,128]{1,0:T(8,128)(2,1)S(1)} %get-tuple-element.28.refs_0_), channel_id=1, source_target_pairs={{0,32},{1,33},{2,34},{3,35},{4,36},{5,37},{6,38},{7,39},{8,40},{9,... | collective-permute-start | bytes 786440 | tf_op jit(solution)/shard_map/ppermute | solution.py:43
  37.7 27.3 %collective-permute-start.8 = (bf16[1024,128]{1,0:T(8,128)(2,1)S(1)}, bf16[1024,128]{1,0:T(8,128)(2,1)S(1)}, u32[]{:S(2)}, u32[]{:S(2)}) collective-permute-start(bf16[1024,128]{1,0:T(8,128)(2,1)S(1)} %get-tuple-element.28.refs_0_), channel_id=1, source_target_pairs={{0,8},{1,9},{2,10},{3,11},{4,12},{5,13},{6,14},{7,15},{8,16},{9,17... | collective-permute-start | bytes 786440 | tf_op jit(solution)/shard_map/ppermute | solution.py:43
  39.7 25.3 %collective-permute-start.9 = (bf16[1024,128]{1,0:T(8,128)(2,1)S(1)}, bf16[1024,128]{1,0:T(8,128)(2,1)S(1)}, u32[]{:S(2)}, u32[]{:S(2)}) collective-permute-start(bf16[1024,128]{1,0:T(8,128)(2,1)S(1)} %get-tuple-element.28.refs_0_), channel_id=1, source_target_pairs={{0,24},{1,25},{2,26},{3,27},{4,28},{5,29},{6,30},{7,31},{8,0},{9,1... | collective-permute-start | bytes 786440 | tf_op jit(solution)/shard_map/ppermute | solution.py:43
  41.9 23.1 %collective-permute-start.11 = (bf16[1024,128]{1,0:T(8,128)(2,1)S(1)}, bf16[1024,128]{1,0:T(8,128)(2,1)S(1)}, u32[]{:S(2)}, u32[]{:S(2)}) collective-permute-start(bf16[1024,128]{1,0:T(8,128)(2,1)S(1)} %slice.16.refs_1_), channel_id=1, source_target_pairs={{0,8},{1,9},{2,10},{3,11},{4,12},{5,13},{6,14},{7,15},{8,16},{9,17... | collective-permute-start | bytes 786440 | tf_op jit(solution)/shard_map/ppermute | solution.py:43
  41.9 23.1 %collective-permute-start.12 = (bf16[1024,128]{1,0:T(8,128)(2,1)S(1)}, bf16[1024,128]{1,0:T(8,128)(2,1)S(1)}, u32[]{:S(2)}, u32[]{:S(2)}) collective-permute-start(bf16[1024,128]{1,0:T(8,128)(2,1)S(1)} %slice.16.refs_1_), channel_id=1, source_target_pairs={{0,24},{1,25},{2,26},{3,27},{4,28},{5,29},{6,30},{7,31},{8,0},{9,1... | collective-permute-start | bytes 786440 | tf_op jit(solution)/shard_map/ppermute | solution.py:43
  65.1 10.6 %collective-permute-start.15 = (bf16[2048,128]{1,0:T(8,128)(2,1)S(1)}, bf16[2048,128]{1,0:T(8,128)(2,1)S(1)}, u32[]{:S(2)}, u32[]{:S(2)}) collective-permute-start(bf16[2048,128]{1,0:T(8,128)(2,1)S(1)} %bitcast.19), channel_id=1, source_target_pairs={{0,8},{1,9},{2,10},{3,11},{4,12},{5,13},{6,14},{7,15},{8,16},{9,17... | collective-permute-start | bytes 1572872 | tf_op jit(solution)/shard_map/ppermute | solution.py:43
  65.5 10.3 %collective-permute-start.18 = (bf16[1024,128]{1,0:T(8,128)(2,1)S(1)}, bf16[1024,128]{1,0:T(8,128)(2,1)S(1)}, u32[]{:S(2)}, u32[]{:S(2)}) collective-permute-start(bf16[1024,128]{1,0:T(8,128)(2,1)S(1)} %collective-permute-done.9.refs_1_), channel_id=1, source_target_pairs={{0,32},{1,33},{2,34},{3,35},{4,36},{5,37},{6,38},{7,39},{8,40},{9,... | collective-permute-start | bytes 786440 | tf_op jit(solution)/shard_map/ppermute | solution.py:43
  66.0 9.8 %collective-permute-start.19 = (bf16[1024,128]{1,0:T(8,128)(2,1)S(1)}, bf16[1024,128]{1,0:T(8,128)(2,1)S(1)}, u32[]{:S(2)}, u32[]{:S(2)}) collective-permute-start(bf16[1024,128]{1,0:T(8,128)(2,1)S(1)} %collective-permute-done.11.refs_2_), channel_id=1, source_target_pairs={{0,32},{1,33},{2,34},{3,35},{4,36},{5,37},{6,38},{7,39},{8,40},{9,... | collective-permute-start | bytes 786440 | tf_op jit(solution)/shard_map/ppermute | solution.py:43
  66.1 9.7 %collective-permute-start.20 = (bf16[1024,128]{1,0:T(8,128)(2,1)S(1)}, bf16[1024,128]{1,0:T(8,128)(2,1)S(1)}, u32[]{:S(2)}, u32[]{:S(2)}) collective-permute-start(bf16[1024,128]{1,0:T(8,128)(2,1)S(1)} %collective-permute-done.12.refs_3_), channel_id=1, source_target_pairs={{0,32},{1,33},{2,34},{3,35},{4,36},{5,37},{6,38},{7,39},{8,40},{9,... | collective-permute-start | bytes 786440 | tf_op jit(solution)/shard_map/ppermute | solution.py:43
  67.0 33.9 %collective-permute-start.24 = (bf16[128,1024]{1,0:T(8,128)(2,1)S(1)}, bf16[128,1024]{1,0:T(8,128)(2,1)S(1)}, u32[]{:S(2)}, u32[]{:S(2)}) collective-permute-start(bf16[128,1024]{1,0:T(8,128)(2,1)S(1)} %copy-done.1), channel_id=1, source_target_pairs={{0,1},{1,0},{2,3},{3,2},{4,5},{5,4},{6,7},{7,6},{8,9},{9,8},{10,11... | collective-permute-start | bytes 786440 | tf_op jit(solution)/shard_map/ppermute | solution.py:43
  75.8 12.4 %collective-permute-start.16 = (bf16[2048,128]{1,0:T(8,128)(2,1)S(1)}, bf16[2048,128]{1,0:T(8,128)(2,1)S(1)}, u32[]{:S(2)}, u32[]{:S(2)}) collective-permute-start(bf16[2048,128]{1,0:T(8,128)(2,1)S(1)} %collective-permute-done.15.refs_0_), channel_id=1, source_target_pairs={{0,32},{1,33},{2,34},{3,35},{4,36},{5,37},{6,38},{7,39},{8,40},{9,... | collective-permute-start | bytes 1572872 | tf_op jit(solution)/shard_map/ppermute | solution.py:43
  91.4 7.7 %collective-permute-start.21 = (bf16[512,128]{1,0:T(8,128)(2,1)S(1)}, bf16[512,128]{1,0:T(8,128)(2,1)S(1)}, u32[]{:S(2)}, u32[]{:S(2)}) collective-permute-start(bf16[512,128]{1,0:T(8,128)(2,1)S(1)} %shard_map.57), channel_id=1, source_target_pairs={{0,64},{1,65},{2,66},{3,67},{4,68},{5,69},{6,70},{7,71},{8,72},{9,... | collective-permute-start | bytes 393224 | tf_op jit(solution)/shard_map/ppermute | solution.py:43
  99.1 7.6 %collective-permute-start.23 = (bf16[512,128]{1,0:T(8,128)(2,1)S(1)}, bf16[512,128]{1,0:T(8,128)(2,1)S(1)}, u32[]{:S(2)}, u32[]{:S(2)}) collective-permute-start(bf16[512,128]{1,0:T(8,128)(2,1)S(1)} %collective-permute-done.21.refs_1_), channel_id=1, source_target_pairs={{0,1},{1,0},{2,3},{3,2},{4,5},{5,4},{6,7},{7,6},{8,9},{9,8},{10,11... | collective-permute-start | bytes 393224 | tf_op jit(solution)/shard_map/ppermute | solution.py:43
  108.4 14.5 %collective-permute-start.25 = (bf16[1024,128]{1,0:T(8,128)(2,1)S(1)}, bf16[1024,128]{1,0:T(8,128)(2,1)S(1)}, u32[]{:S(2)}, u32[]{:S(2)}) collective-permute-start(bf16[1024,128]{1,0:T(8,128)(2,1)S(1)} %get-tuple-element.44), channel_id=1, source_target_pairs={{0,2},{1,3},{2,4},{3,5},{4,6},{5,7},{6,0},{7,1},{8,10},{9,11},{10,... | collective-permute-start | bytes 786440 | tf_op jit(solution)/shard_map/ppermute | solution.py:43
  109.3 13.5 %collective-permute-start.26 = (bf16[1024,128]{1,0:T(8,128)(2,1)S(1)}, bf16[1024,128]{1,0:T(8,128)(2,1)S(1)}, u32[]{:S(2)}, u32[]{:S(2)}) collective-permute-start(bf16[1024,128]{1,0:T(8,128)(2,1)S(1)} %get-tuple-element.45), channel_id=1, source_target_pairs={{0,4},{1,5},{2,6},{3,7},{4,0},{5,1},{6,2},{7,3},{8,12},{9,13},{10,... | collective-permute-start | bytes 786440 | tf_op jit(solution)/shard_map/ppermute | solution.py:43
  110.9 12.5 %collective-permute-start.27 = (bf16[1024,128]{1,0:T(8,128)(2,1)S(1)}, bf16[1024,128]{1,0:T(8,128)(2,1)S(1)}, u32[]{:S(2)}, u32[]{:S(2)}) collective-permute-start(bf16[1024,128]{1,0:T(8,128)(2,1)S(1)} %get-tuple-element.46), channel_id=1, source_target_pairs={{0,6},{1,7},{2,0},{3,1},{4,2},{5,3},{6,4},{7,5},{8,14},{9,15},{10,... | collective-permute-start | bytes 786440 | tf_op jit(solution)/shard_map/ppermute | solution.py:43
  (8 other events, 49.8 us)

commit v3 on v2

--- a/solution.py
+++ b/solution.py
@@ -58,7 +58,7 @@
 def project_kernel(ids_ref, *refs):
     x_refs = refs[:7]
     halves = refs[7:9]
-    gain_ref, w_ref, kv_ref, q_ref, out_ref, n_even, n_odd = refs[9:]
+    gain_ref, w_ref, kv_ref, q_ref, out_ref, qout_ref, n_even, n_odd = refs[9:]
     tok = x_refs[0].shape[0]
     step = 128
     half = tok // 2
@@ -109,7 +109,7 @@
             qkeep = jnp.where(par > 0, qt[HD:], qt[:HD])
             qgive = jnp.where(par > 0, qt[:HD], qt[HD:])
             q_ref[block : block + HD, :] = qkeep.astype(bf16)
-            out_ref[tok + block : tok + block + HD, :] = qgive.astype(bf16)
+            qout_ref[block : block + HD, :] = qgive.astype(bf16)
 
     bufs = (n_even, n_odd)
     trips = half // step
@@ -151,10 +151,11 @@
         out_shape=(
             jax.ShapeDtypeStruct((tok, 128), bf16),
             jax.ShapeDtypeStruct((tok // 2, 128), bf16),
-            jax.ShapeDtypeStruct((tok + tok // 2, 128), bf16),
+            jax.ShapeDtypeStruct((tok, 128), bf16),
+            jax.ShapeDtypeStruct((tok // 2, 128), bf16),
         ),
         in_specs=[smem()] + [vmem()] * 11,
-        out_specs=(vmem(), vmem(), vmem()),
+        out_specs=(vmem(), vmem(), vmem(), vmem()),
         scratch_shapes=[
             pltpu.VMEM((8, 256, 128), bf16),
             pltpu.VMEM((8, 256, 128), bf16),
@@ -344,48 +345,94 @@
     )(*args)
 
 
-def mix_kernel(pos_ref, *refs):
-    kept, back, peer_kept, peer_back = refs[:4]
+def columns_of(att_refs, t, swap):
+    kept, back, peer_kept, peer_back = att_refs
+    at = pl.ds(pl.multiple_of(t * HD, HD), HD)
+    cols = []
+    for mine, other in ((kept, back), (peer_kept, peer_back)):
+        a, b = mine[at, :], other[at, :]
+        cols += [jnp.where(swap, b, a), jnp.where(swap, a, b)]
+    return jnp.concatenate(cols, axis=0).T
+
+
+def weights_for(pos_ref, own_ref, peer_ref, w_ref, steps):
+    for n, b in enumerate(steps):
+        cols = pl.ds(pl.multiple_of((((pos_ref[0] + b) % 4) * 2 + pos_ref[1]) * 128, 128), 128)
+        w_ref[0:128, n * 128 : (n + 1) * 128] = own_ref[:, cols]
+        w_ref[128:256, n * 128 : (n + 1) * 128] = peer_ref[:, cols]
+
+
+def far_kernel(pos_ref, *refs):
+    att_refs, (own_ref, peer_ref, lo_ref, hi_ref, t_ref, w_ref) = refs[:4], refs[4:]
+    weights_for(pos_ref, own_ref, peer_ref, w_ref, (2,))
     swap = pos_ref[2] > 0
-    own_ref, peer_ref, x_ref, bias_ref = refs[4:8]
-    base_ref = refs[8]
-    out_refs = refs[9:12]
-    w_ref = refs[12]
-    for b in range(4):
-        cols = pl.ds(pl.multiple_of((((pos_ref[0] + b) % 4) * 2 + pos_ref[1]) * 128, 128), 128)
-        w_ref[0:128, b * 128 : (b + 1) * 128] = own_ref[:, cols]
-        w_ref[128:256, b * 128 : (b + 1) * 128] = peer_ref[:, cols]
-
-    count = kept.shape[0] // HD
+    count = att_refs[0].shape[0] // HD
+    for t in range(count):
+        rows = columns_of(att_refs, t, swap)
+        t_ref[t] = rows
+        out = jnp.dot(rows, w_ref[...], preferred_element_type=f32).astype(bf16)
+        half = (lo_ref, hi_ref)[t // (count // 2)]
+        to = (t % (count // 2)) * 128
+        half[to : to + 128, :] = out
+
+
+def mix_far(pos, att, own, peer):
+    tok = att[0].shape[0] * 2
+    return pl.pallas_call(
+        far_kernel,
+        out_shape=[jax.ShapeDtypeStruct((tok // 2, 128), bf16)] * 2
+        + [jax.ShapeDtypeStruct((tok // 128, 128, 256), bf16)],
+        in_specs=[smem()] + [vmem()] * 6,
+        out_specs=[vmem()] * 3,
+        scratch_shapes=[pltpu.VMEM((256, 128), bf16)],
+        compiler_params=pltpu.CompilerParams(vmem_limit_bytes=6 << 20),
+        name="mix_far",
+    )(pos, *att, own, peer)
+
+
+def mix_kernel(pos_ref, rows_ref, own_ref, peer_ref, x_ref, bias_ref, base_ref, up_ref, down_ref, w_ref):
+    weights_for(pos_ref, own_ref, peer_ref, w_ref, (0, 1, 3))
 
     def one(t, _):
-        at = pl.ds(pl.multiple_of(t * HD, HD), HD)
-        cols = []
-        for mine, other in ((kept, back), (peer_kept, peer_back)):
-            a, b = mine[at, :], other[at, :]
-            cols += [jnp.where(swap, b, a), jnp.where(swap, a, b)]
-        rows = jnp.concatenate(cols, axis=0).T
-        out = jnp.dot(rows, w_ref[...], preferred_element_type=f32)
+        out = jnp.dot(rows_ref[t], w_ref[...], preferred_element_type=f32)
         to = pl.ds(pl.multiple_of(t * 128, 128), 128)
         base_ref[to, :] = out[:, :128] + x_ref[to, :].astype(f32) + bias_ref[...]
-        for b in range(3):
-            out_refs[b][to, :] = out[:, (b + 1) * 128 : (b + 2) * 128].astype(bf16)
+        up_ref[to, :] = out[:, 128:256].astype(bf16)
+        down_ref[to, :] = out[:, 256:].astype(bf16)
         return 0
 
-    lax.fori_loop(0, count, one, 0, unroll=2)
-
-
-def mix(pos, att, own, peer, x, bias):
-    tok = att[0].shape[0] * 2
+    lax.fori_loop(0, rows_ref.shape[0], one, 0, unroll=4)
+
+
+def mix(pos, rows, own, peer, x, bias):
     return pl.pallas_call(
         mix_kernel,
-        out_shape=[jax.ShapeDtypeStruct((tok, 128), f32)] + [jax.ShapeDtypeStruct((tok, 128), bf16)] * 3,
-        in_specs=[smem()] + [vmem()] * 8,
-        out_specs=[vmem()] * 4,
-        scratch_shapes=[pltpu.VMEM((256, 512), bf16)],
+        out_shape=[jax.ShapeDtypeStruct(x.shape, f32)] + [jax.ShapeDtypeStruct(x.shape, bf16)] * 2,
+        in_specs=[smem()] + [vmem()] * 5,
+        out_specs=[vmem()] * 3,
+        scratch_shapes=[pltpu.VMEM((256, 384), bf16)],
         compiler_params=pltpu.CompilerParams(vmem_limit_bytes=6 << 20),
         name="mix",
-    )(pos, *att, own, peer, x, bias)
+    )(pos, rows, own, peer, x, bias)
+
+
+def join_kernel(up_ref, down_ref, lo_ref, hi_ref, upo_ref, downo_ref):
+    half = lo_ref.shape[0]
+    upo_ref[:half] = (up_ref[:half].astype(f32) + lo_ref[...].astype(f32)).astype(bf16)
+    upo_ref[half:] = up_ref[half:]
+    downo_ref[:half] = down_ref[:half]
+    downo_ref[half:] = (down_ref[half:].astype(f32) + hi_ref[...].astype(f32)).astype(bf16)
+
+
+def join(up, down, lo, hi):
+    return pl.pallas_call(
+        join_kernel,
+        out_shape=[jax.ShapeDtypeStruct(up.shape, bf16)] * 2,
+        in_specs=[vmem()] * 4,
+        out_specs=[vmem()] * 2,
+        compiler_params=pltpu.CompilerParams(vmem_limit_bytes=6 << 20),
+        name="join",
+    )(up, down, lo, hi)
 
 
 def per_device(tokens, ln_gain, w_qkv, w_out, out_bias):
@@ -409,16 +456,16 @@
     xs = jnp.stack([x, (x + 3) % 4, (x + 1) % 4, (x + 2) % 4])
     ids = jnp.concatenate([xs[:3] * 2 + yl, xs * 2 + 1 - yl, xs[3:] * 2 + yl, yh.reshape(1)]).astype(jnp.int32)
 
-    kv, q, give = project(ids, blocks, ln_gain.reshape(8, 1, 128), w_held)
-    got = send(give, YH_SWAP)
+    kv, q, give, give_q = project(ids, blocks, ln_gain.reshape(8, 1, 128), w_held)
+    kf = send(give, YH_SWAP)
+    q_far = send(give_q, YH_SWAP)
     k_other = send(kv, CORE_SWAP)
     k_up = send(kv, Z_UP)
     k_down = send(kv, Z_DOWN)
-    kf = got[:tok]
     f_other = send(kf, CORE_SWAP)
     f_up = send(kf, Z_UP)
     f_down = send(kf, Z_DOWN)
-    qs = ((got, (tok, tok // 2)), (q, (0, tok // 2)))
+    qs = ((q_far, (0, tok // 2)), (q, (0, tok // 2)))
     state = attend((kv, kf, k_other, f_other), qs)
     k_up, k_down, f_up, f_down, w_send, state = lax.optimization_barrier((k_up, k_down, f_up, f_down, w_out, state))
     chosen = jnp.where(rows % 2 > 0, jnp.stack([k_down, f_down]), jnp.stack([k_up, f_up]))
@@ -435,11 +482,14 @@
     peer = send(att, YL_SWAP)
     peer_back = send(back, YL_SWAP)
     pos = jnp.stack([x, yl, yh]).astype(jnp.int32)
-    parts = mix(pos, (att, back, peer, peer_back), w_out, w_peer, tokens, out_bias.reshape(1, 128))
-    up = send(parts[1], X_UP)
-    across = send(parts[2], X_FAR)
-    down = send(parts[3], X_DOWN)
-    return (parts[0] + up.astype(f32) + across.astype(f32) + down.astype(f32)).astype(bf16)
+    lo, hi, att_rows = mix_far(pos, (att, back, peer, peer_back), w_out, w_peer)
+    lo = send(lo, X_UP)
+    hi = send(hi, X_DOWN)
+    base, up, down = mix(pos, att_rows, w_out, w_peer, tokens, out_bias.reshape(1, 128))
+    up, down = join(up, down, lo, hi)
+    up = send(up, X_UP)
+    down = send(down, X_DOWN)
+    return (base + up.astype(f32) + down.astype(f32)).astype(bf16)
 
 
 def solution(mesh):

time: 125 us -> 124 us (level)
  waiting for transfers between devices: 40.4 us -> 32.9 us
  starting transfers between devices: 37.9 us -> 43.5 us
    ppermute x28 -> x30, waiting for transfers between devices: 40.4 us -> 32.9 us  [send(): return lax.ppermute(x, AXES, pairs)]
    ppermute x28 -> x30, starting transfers between devices: 37.9 us -> 43.5 us  [send(): return lax.ppermute(x, AXES, pairs)]
  transfers between devices with their start and end apart: 28 -> 30, of which waited for: 10 -> 11; matrix products, arithmetic and copies ran while one was open for 0% -> 0% of each run, Pallas kernels for 32% -> 33%
where the time goes in v3:
time: 124 us
  Pallas kernels  45 us (36%)
  starting transfers between devices  43.5 us (35%)
  waiting for transfers between devices  32.9 us (27%)
    ppermute x30, starting transfers between devices, send(): return lax.ppermute(x, AXES, pairs)  43.5 us
    pallas_call x4, Pallas kernels, attend(): pl.pallas_call(functools.partial(attend_kernel, npieces=len(pieces), wind...  38.6 us
    ppermute x30, waiting for transfers between devices, send(): return lax.ppermute(x, AXES, pairs)  32.9 us
    pallas_call x1, Pallas kernels, project(): pl.pallas_call(project_kernel, out_shape=(jax.ShapeDtypeStruct((tok, 128)...  3.01 us
  transfers between devices with their start and end apart: 30, of which 11 were waited for; matrix products, arithmetic and copies ran while one was open for 0% of the time, Pallas kernels for 33%

profile of v3, /device:TPU:0, one launch (start us, length us, event | category | flops | bytes accessed | tf_op | source)
XLA Modules:
  0.0 123.5 jit_solution(5450120313441396850)
XLA Ops:
  4.9 4.5 %collective-permute-done.refs_1_ = bf16[1024,128]{1,0:T(8,128)(2,1)S(1)} collective-permute-done((bf16[1024,128]{1,0:T(8,128)(2,1)}, bf16[1024,128]{1,0:T(8,128)(2,1)S(1)}, u32[]{:S(2)}, u32[]{:S(2)}) %collective-permute-start) | collective-permute-done | bytes 262176 | tf_op jit(solution)/shard_map/ppermute | solution.py:43
  9.4 1.8 %collective-permute-start.3 = (bf16[1024,128]{1,0:T(8,128)(2,1)S(1)}, bf16[1024,128]{1,0:T(8,128)(2,1)S(1)}, u32[]{:S(2)}, u32[]{:S(2)}) collective-permute-start(bf16[1024,128]{1,0:T(8,128)(2,1)S(1)} %collective-permute-done.refs_1_), channel_id=1, source_target_pairs={{0,1},{1,0},{2,3},{3,2},{4,5},{5,4},{6,7},{7,6},{8,9},{9,8},{10,11... | collective-permute-start | bytes 786440 | tf_op jit(solution)/shard_map/ppermute | solution.py:43
  11.4 2.5 %collective-permute-start.5 = (bf16[1024,128]{1,0:T(8,128)(2,1)S(1)}, bf16[1024,128]{1,0:T(8,128)(2,1)S(1)}, u32[]{:S(2)}, u32[]{:S(2)}) collective-permute-start(bf16[1024,128]{1,0:T(8,128)(2,1)S(1)} %collective-permute-done.2.refs_3_), channel_id=1, source_target_pairs={{0,4},{1,5},{2,6},{3,7},{4,0},{5,1},{6,2},{7,3},{8,12},{9,13},{10,... | collective-permute-start | bytes 786440 | tf_op jit(solution)/shard_map/ppermute | solution.py:43
  15.1 2.2 %collective-permute-start.7 = (bf16[512,128]{1,0:T(8,128)(2,1)S(1)}, bf16[512,128]{1,0:T(8,128)(2,1)S(1)}, u32[]{:S(2)}, u32[]{:S(2)}) collective-permute-start(bf16[512,128]{1,0:T(8,128)(2,1)S(1)} %slice.11), channel_id=1, source_target_pairs={{0,6},{1,7},{2,0},{3,1},{4,2},{5,3},{6,4},{7,5},{8,14},{9,15},{10,... | collective-permute-start | bytes 393224 | tf_op jit(solution)/shard_map/ppermute | solution.py:43
  18.8 3.7 %collective-permute-done.6.refs_7_ = bf16[512,128]{1,0:T(8,128)(2,1)S(1)} collective-permute-done((bf16[512,128]{1,0:T(8,128)(2,1)S(1)}, bf16[512,128]{1,0:T(8,128)(2,1)S(1)}, u32[]{:S(2)}, u32[]{:S(2)}) %collective-permute-start.6) | collective-permute-done | bytes 131104 | tf_op jit(solution)/shard_map/ppermute | solution.py:43
  22.5 3.0 %project.1 = (bf16[1024,128]{1,0:T(8,128)(2,1)S(1)}, bf16[512,128]{1,0:T(8,128)(2,1)S(1)}, bf16[1024,128]{1,0:T(8,128)(2,1)S(1)}, bf16[512,128]{1,0:T(8,128)(2,1)S(1)}) custom-call(s32[9]{0:T(128)S(1)} %pad_add_fusion.1.ids_ref, bf16[1024,128]{1,0:T(8,128)(2,1)S(1)} %get-tuple-element.31.refs_0_, bf16[1024,128]{1,0:T(8,128)(2,1)S(1)} %collective-permute-done.refs_1_, ...), custom_call_target="tpu_custom_call" | custom-call | tf_op jit(solution)/shard_map/project/pallas_call | solution.py:149
  25.5 3.4 %collective-permute-start.10 = (bf16[1024,128]{1,0:T(8,128)(2,1)S(1)}, bf16[1024,128]{1,0:T(8,128)(2,1)S(1)}, u32[]{:S(2)}, u32[]{:S(2)}) collective-permute-start(bf16[1024,128]{1,0:T(8,128)(2,1)S(1)} %get-tuple-element.34), channel_id=1, source_target_pairs={{0,64},{1,65},{2,66},{3,67},{4,68},{5,69},{6,70},{7,71},{8,72},{9,... | collective-permute-start | bytes 786440 | tf_op jit(solution)/shard_map/ppermute | solution.py:43
  28.9 5.9 %collective-permute-done.10.refs_1_ = bf16[1024,128]{1,0:T(8,128)(2,1)S(1)} collective-permute-done((bf16[1024,128]{1,0:T(8,128)(2,1)S(1)}, bf16[1024,128]{1,0:T(8,128)(2,1)S(1)}, u32[]{:S(2)}, u32[]{:S(2)}) %collective-permute-start.10) | collective-permute-done | bytes 262176 | tf_op jit(solution)/shard_map/ppermute | solution.py:43
  34.8 3.2 %collective-permute-start.15 = (bf16[512,128]{1,0:T(8,128)(2,1)S(1)}, bf16[512,128]{1,0:T(8,128)(2,1)S(1)}, u32[]{:S(2)}, u32[]{:S(2)}) collective-permute-start(bf16[512,128]{1,0:T(8,128)(2,1)S(1)} %get-tuple-element.35), channel_id=1, source_target_pairs={{0,64},{1,65},{2,66},{3,67},{4,68},{5,69},{6,70},{7,71},{8,72},{9,... | collective-permute-start | bytes 393224 | tf_op jit(solution)/shard_map/ppermute | solution.py:43
  38.1 1.9 %collective-permute-start.8 = (bf16[1024,128]{1,0:T(8,128)(2,1)S(1)}, bf16[1024,128]{1,0:T(8,128)(2,1)S(1)}, u32[]{:S(2)}, u32[]{:S(2)}) collective-permute-start(bf16[1024,128]{1,0:T(8,128)(2,1)S(1)} %get-tuple-element.33.refs_0_), channel_id=1, source_target_pairs={{0,8},{1,9},{2,10},{3,11},{4,12},{5,13},{6,14},{7,15},{8,16},{9,17... | collective-permute-start | bytes 786440 | tf_op jit(solution)/shard_map/ppermute | solution.py:43
  40.0 2.1 %collective-permute-start.9 = (bf16[1024,128]{1,0:T(8,128)(2,1)S(1)}, bf16[1024,128]{1,0:T(8,128)(2,1)S(1)}, u32[]{:S(2)}, u32[]{:S(2)}) collective-permute-start(bf16[1024,128]{1,0:T(8,128)(2,1)S(1)} %get-tuple-element.33.refs_0_), channel_id=1, source_target_pairs={{0,24},{1,25},{2,26},{3,27},{4,28},{5,29},{6,30},{7,31},{8,0},{9,1... | collective-permute-start | bytes 786440 | tf_op jit(solution)/shard_map/ppermute | solution.py:43
  42.2 1.9 %collective-permute-start.11 = (bf16[1024,128]{1,0:T(8,128)(2,1)S(1)}, bf16[1024,128]{1,0:T(8,128)(2,1)S(1)}, u32[]{:S(2)}, u32[]{:S(2)}) collective-permute-start(bf16[1024,128]{1,0:T(8,128)(2,1)S(1)} %collective-permute-done.10.refs_1_), channel_id=1, source_target_pairs={{0,8},{1,9},{2,10},{3,11},{4,12},{5,13},{6,14},{7,15},{8,16},{9,17... | collective-permute-start | bytes 786440 | tf_op jit(solution)/shard_map/ppermute | solution.py:43
  44.1 2.1 %collective-permute-start.12 = (bf16[1024,128]{1,0:T(8,128)(2,1)S(1)}, bf16[1024,128]{1,0:T(8,128)(2,1)S(1)}, u32[]{:S(2)}, u32[]{:S(2)}) collective-permute-start(bf16[1024,128]{1,0:T(8,128)(2,1)S(1)} %collective-permute-done.10.refs_1_), channel_id=1, source_target_pairs={{0,24},{1,25},{2,26},{3,27},{4,28},{5,29},{6,30},{7,31},{8,0},{9,1... | collective-permute-start | bytes 786440 | tf_op jit(solution)/shard_map/ppermute | solution.py:43
  46.3 19.8 %shard_map.55 = (f32[4,72,512]{2,1,0:T(8,128)S(1)}, f32[4,1,512]{2,1,0:T(1,128)S(1)}) custom-call(bf16[1024,128]{1,0:T(8,128)(2,1)S(1)} %get-tuple-element.33.refs_0_, bf16[1024,128]{1,0:T(8,128)(2,1)S(1)} %collective-permute-done.10.refs_1_, bf16[1024,128]{1,0:T(8,128)(2,1)S(1)} %collective-permute-done.13.refs_2_, ...), custom_call_target="tpu_custom_call" | custom-call | flops 4294967296 | bytes 1048576 | tf_op jit(solution)/shard_map/pallas_call | solution.py:335
  70.2 6.7 %collective-permute-done.16.refs_0_ = bf16[2048,128]{1,0:T(8,128)(2,1)S(1)} collective-permute-done((bf16[2048,128]{1,0:T(8,128)(2,1)S(1)}, bf16[2048,128]{1,0:T(8,128)(2,1)S(1)}, u32[]{:S(2)}, u32[]{:S(2)}) %collective-permute-start.16) | collective-permute-done | bytes 524320 | tf_op jit(solution)/shard_map/ppermute | solution.py:43
  76.9 12.3 %shard_map.56 = (f32[4,72,512]{2,1,0:T(8,128)S(1)}, f32[4,1,512]{2,1,0:T(1,128)S(1)}) custom-call(bf16[1024,128]{1,0:T(8,128)(2,1)S(1)} %collective-permute-done.8.refs_0_, bf16[1024,128]{1,0:T(8,128)(2,1)S(1)} %collective-permute-done.9.refs_1_, bf16[1024,128]{1,0:T(8,128)(2,1)S(1)} %collective-permute-done.11.refs_2_, ...), custom_call_target="tpu_custom_call" | custom-call | flops 8589934592 | bytes 2097152 | tf_op jit(solution)/shard_map/pallas_call | solution.py:335
  89.2 3.2 %shard_map.57 = bf16[512,128]{1,0:T(8,128)(2,1)S(1)} custom-call(bf16[2048,128]{1,0:T(8,128)(2,1)S(1)} %collective-permute-done.16.refs_0_, bf16[2048,128]{1,0:T(8,128)(2,1)S(1)} %collective-permute-done.17.refs_1_, bf16[512,128]{1,0:T(8,128)(2,1)S(1)} %collective-permute-done.15.refs_4_.refs_8_.refs_2_, f32[4,72,512]{2,1,0:T(8,128)S(1)} %get-tuple-element.45.refs_3_, ...), custom_call_target="tpu_custom_call" | custom-call | flops 2147483648 | bytes 1048576 | tf_op jit(solution)/shard_map/pallas_call | solution.py:335
  92.5 3.5 %collective-permute-start.22 = (bf16[512,128]{1,0:T(8,128)(2,1)S(1)}, bf16[512,128]{1,0:T(8,128)(2,1)S(1)}, u32[]{:S(2)}, u32[]{:S(2)}) collective-permute-start(bf16[512,128]{1,0:T(8,128)(2,1)S(1)} %shard_map.57), channel_id=1, source_target_pairs={{0,64},{1,65},{2,66},{3,67},{4,68},{5,69},{6,70},{7,71},{8,72},{9,... | collective-permute-start | bytes 393224 | tf_op jit(solution)/shard_map/ppermute | solution.py:43
  96.0 3.2 %shard_map.58.refs_0_ = bf16[512,128]{1,0:T(8,128)(2,1)S(1)} custom-call(bf16[2048,128]{1,0:T(8,128)(2,1)S(1)} %collective-permute-done.16.refs_0_, bf16[2048,128]{1,0:T(8,128)(2,1)S(1)} %collective-permute-done.17.refs_1_, bf16[512,128]{1,0:T(8,128)(2,1)S(1)} %get-tuple-element.47.refs_5_.refs_9_.refs_2_, f32[4,72,512]{2,1,0:T(8,128)S(1)} %get-tuple-element.45.refs_3_, ...), custom_call_target="tpu_custom_call" | custom-call | flops 2147483648 | bytes 1048576 | tf_op jit(solution)/shard_map/pallas_call | solution.py:335
  102.0 3.7 %collective-permute-done.23.refs_2_ = bf16[512,128]{1,0:T(8,128)(2,1)S(1)} collective-permute-done((bf16[512,128]{1,0:T(8,128)(2,1)S(1)}, bf16[512,128]{1,0:T(8,128)(2,1)S(1)}, u32[]{:S(2)}, u32[]{:S(2)}) %collective-permute-start.23) | collective-permute-done | bytes 131104 | tf_op jit(solution)/shard_map/ppermute | solution.py:43
  105.7 2.1 %collective-permute-done.24.refs_3_ = bf16[512,128]{1,0:T(8,128)(2,1)S(1)} collective-permute-done((bf16[512,128]{1,0:T(8,128)(2,1)S(1)}, bf16[512,128]{1,0:T(8,128)(2,1)S(1)}, u32[]{:S(2)}, u32[]{:S(2)}) %collective-permute-start.24) | collective-permute-done | bytes 131104 | tf_op jit(solution)/shard_map/ppermute | solution.py:43
  109.7 2.3 %collective-permute-start.27 = (bf16[512,128]{1,0:T(8,128)(2,1)S(1)}, bf16[512,128]{1,0:T(8,128)(2,1)S(1)}, u32[]{:S(2)}, u32[]{:S(2)}) collective-permute-start(bf16[512,128]{1,0:T(8,128)(2,1)S(1)} %get-tuple-element.54), channel_id=1, source_target_pairs={{0,6},{1,7},{2,0},{3,1},{4,2},{5,3},{6,4},{7,5},{8,14},{9,15},{10,... | collective-permute-start | bytes 393224 | tf_op jit(solution)/shard_map/ppermute | solution.py:43
  116.2 2.2 %collective-permute-start.29 = (bf16[1024,128]{1,0:T(8,128)(2,1)S(1)}, bf16[1024,128]{1,0:T(8,128)(2,1)S(1)}, u32[]{:S(2)}, u32[]{:S(2)}) collective-permute-start(bf16[1024,128]{1,0:T(8,128)(2,1)S(1)} %get-tuple-element.56), channel_id=1, source_target_pairs={{0,6},{1,7},{2,0},{3,1},{4,2},{5,3},{6,4},{7,5},{8,14},{9,15},{10,... | collective-permute-start | bytes 786440 | tf_op jit(solution)/shard_map/ppermute | solution.py:43
  118.4 4.3 %collective-permute-done.28 = bf16[1024,128]{1,0:T(8,128)(2,1)S(1)} collective-permute-done((bf16[1024,128]{1,0:T(8,128)(2,1)S(1)}, bf16[1024,128]{1,0:T(8,128)(2,1)S(1)}, u32[]{:S(2)}, u32[]{:S(2)}) %collective-permute-start.28) | collective-permute-done | bytes 262176 | tf_op jit(solution)/shard_map/ppermute | solution.py:43
  (61 shorter events, 21.6 us)
Async XLA Ops:
  0.0 9.4 %collective-permute-start = (bf16[1024,128]{1,0:T(8,128)(2,1)}, bf16[1024,128]{1,0:T(8,128)(2,1)S(1)}, u32[]{:S(2)}, u32[]{:S(2)}) collective-permute-start(bf16[1024,128]{1,0:T(8,128)(2,1)} %x_ref.3), channel_id=1, source_target_pairs={{0,2},{1,3},{2,4},{3,5},{4,6},{5,7},{6,0},{7,1},{8,10},{9,11},{10,... | collective-permute-start | bytes 786440 | tf_op jit(solution)/shard_map/ppermute | solution.py:43
  1.6 9.6 %collective-permute-start.1 = (bf16[1024,128]{1,0:T(8,128)(2,1)}, bf16[1024,128]{1,0:T(8,128)(2,1)S(1)}, u32[]{:S(2)}, u32[]{:S(2)}) collective-permute-start(bf16[1024,128]{1,0:T(8,128)(2,1)} %x_ref.3), channel_id=1, source_target_pairs={{0,6},{1,7},{2,0},{3,1},{4,2},{5,3},{6,4},{7,5},{8,14},{9,15},{10,... | collective-permute-start | bytes 786440 | tf_op jit(solution)/shard_map/ppermute | solution.py:43
  3.2 8.2 %collective-permute-start.2 = (bf16[1024,128]{1,0:T(8,128)(2,1)}, bf16[1024,128]{1,0:T(8,128)(2,1)S(1)}, u32[]{:S(2)}, u32[]{:S(2)}) collective-permute-start(bf16[1024,128]{1,0:T(8,128)(2,1)} %x_ref.3), channel_id=1, source_target_pairs={{0,1},{1,0},{2,3},{3,2},{4,5},{5,4},{6,7},{7,6},{8,9},{9,8},{10,11... | collective-permute-start | bytes 786440 | tf_op jit(solution)/shard_map/ppermute | solution.py:43
  9.4 13.1 %collective-permute-start.3 = (bf16[1024,128]{1,0:T(8,128)(2,1)S(1)}, bf16[1024,128]{1,0:T(8,128)(2,1)S(1)}, u32[]{:S(2)}, u32[]{:S(2)}) collective-permute-start(bf16[1024,128]{1,0:T(8,128)(2,1)S(1)} %collective-permute-done.refs_1_), channel_id=1, source_target_pairs={{0,1},{1,0},{2,3},{3,2},{4,5},{5,4},{6,7},{7,6},{8,9},{9,8},{10,11... | collective-permute-start | bytes 786440 | tf_op jit(solution)/shard_map/ppermute | solution.py:43
  11.2 11.3 %collective-permute-start.4 = (bf16[1024,128]{1,0:T(8,128)(2,1)S(1)}, bf16[1024,128]{1,0:T(8,128)(2,1)S(1)}, u32[]{:S(2)}, u32[]{:S(2)}) collective-permute-start(bf16[1024,128]{1,0:T(8,128)(2,1)S(1)} %collective-permute-done.1.refs_2_), channel_id=1, source_target_pairs={{0,1},{1,0},{2,3},{3,2},{4,5},{5,4},{6,7},{7,6},{8,9},{9,8},{10,11... | collective-permute-start | bytes 786440 | tf_op jit(solution)/shard_map/ppermute | solution.py:43
  11.4 11.1 %collective-permute-start.5 = (bf16[1024,128]{1,0:T(8,128)(2,1)S(1)}, bf16[1024,128]{1,0:T(8,128)(2,1)S(1)}, u32[]{:S(2)}, u32[]{:S(2)}) collective-permute-start(bf16[1024,128]{1,0:T(8,128)(2,1)S(1)} %collective-permute-done.2.refs_3_), channel_id=1, source_target_pairs={{0,4},{1,5},{2,6},{3,7},{4,0},{5,1},{6,2},{7,3},{8,12},{9,13},{10,... | collective-permute-start | bytes 786440 | tf_op jit(solution)/shard_map/ppermute | solution.py:43
  14.0 8.5 %collective-permute-start.6 = (bf16[512,128]{1,0:T(8,128)(2,1)S(1)}, bf16[512,128]{1,0:T(8,128)(2,1)S(1)}, u32[]{:S(2)}, u32[]{:S(2)}) collective-permute-start(bf16[512,128]{1,0:T(8,128)(2,1)S(1)} %slice.10), channel_id=1, source_target_pairs={{0,2},{1,3},{2,4},{3,5},{4,6},{5,7},{6,0},{7,1},{8,10},{9,11},{10,... | collective-permute-start | bytes 393224 | tf_op jit(solution)/shard_map/ppermute | solution.py:43
  25.5 9.3 %collective-permute-start.10 = (bf16[1024,128]{1,0:T(8,128)(2,1)S(1)}, bf16[1024,128]{1,0:T(8,128)(2,1)S(1)}, u32[]{:S(2)}, u32[]{:S(2)}) collective-permute-start(bf16[1024,128]{1,0:T(8,128)(2,1)S(1)} %get-tuple-element.34), channel_id=1, source_target_pairs={{0,64},{1,65},{2,66},{3,67},{4,68},{5,69},{6,70},{7,71},{8,72},{9,... | collective-permute-start | bytes 786440 | tf_op jit(solution)/shard_map/ppermute | solution.py:43
  28.9 15.3 %collective-permute-start.13 = (bf16[1024,128]{1,0:T(8,128)(2,1)S(1)}, bf16[1024,128]{1,0:T(8,128)(2,1)S(1)}, u32[]{:S(2)}, u32[]{:S(2)}) collective-permute-start(bf16[1024,128]{1,0:T(8,128)(2,1)S(1)} %get-tuple-element.33.refs_0_), channel_id=1, source_target_pairs={{0,32},{1,33},{2,34},{3,35},{4,36},{5,37},{6,38},{7,39},{8,40},{9,... | collective-permute-start | bytes 786440 | tf_op jit(solution)/shard_map/ppermute | solution.py:43
  34.8 11.5 %collective-permute-start.14 = (bf16[1024,128]{1,0:T(8,128)(2,1)S(1)}, bf16[1024,128]{1,0:T(8,128)(2,1)S(1)}, u32[]{:S(2)}, u32[]{:S(2)}) collective-permute-start(bf16[1024,128]{1,0:T(8,128)(2,1)S(1)} %collective-permute-done.10.refs_1_), channel_id=1, source_target_pairs={{0,32},{1,33},{2,34},{3,35},{4,36},{5,37},{6,38},{7,39},{8,40},{9,... | collective-permute-start | bytes 786440 | tf_op jit(solution)/shard_map/ppermute | solution.py:43
  34.8 7.4 %collective-permute-start.15 = (bf16[512,128]{1,0:T(8,128)(2,1)S(1)}, bf16[512,128]{1,0:T(8,128)(2,1)S(1)}, u32[]{:S(2)}, u32[]{:S(2)}) collective-permute-start(bf16[512,128]{1,0:T(8,128)(2,1)S(1)} %get-tuple-element.35), channel_id=1, source_target_pairs={{0,64},{1,65},{2,66},{3,67},{4,68},{5,69},{6,70},{7,71},{8,72},{9,... | collective-permute-start | bytes 393224 | tf_op jit(solution)/shard_map/ppermute | solution.py:43
  38.1 28.0 %collective-permute-start.8 = (bf16[1024,128]{1,0:T(8,128)(2,1)S(1)}, bf16[1024,128]{1,0:T(8,128)(2,1)S(1)}, u32[]{:S(2)}, u32[]{:S(2)}) collective-permute-start(bf16[1024,128]{1,0:T(8,128)(2,1)S(1)} %get-tuple-element.33.refs_0_), channel_id=1, source_target_pairs={{0,8},{1,9},{2,10},{3,11},{4,12},{5,13},{6,14},{7,15},{8,16},{9,17... | collective-permute-start | bytes 786440 | tf_op jit(solution)/shard_map/ppermute | solution.py:43
  40.0 26.1 %collective-permute-start.9 = (bf16[1024,128]{1,0:T(8,128)(2,1)S(1)}, bf16[1024,128]{1,0:T(8,128)(2,1)S(1)}, u32[]{:S(2)}, u32[]{:S(2)}) collective-permute-start(bf16[1024,128]{1,0:T(8,128)(2,1)S(1)} %get-tuple-element.33.refs_0_), channel_id=1, source_target_pairs={{0,24},{1,25},{2,26},{3,27},{4,28},{5,29},{6,30},{7,31},{8,0},{9,1... | collective-permute-start | bytes 786440 | tf_op jit(solution)/shard_map/ppermute | solution.py:43
  42.2 23.9 %collective-permute-start.11 = (bf16[1024,128]{1,0:T(8,128)(2,1)S(1)}, bf16[1024,128]{1,0:T(8,128)(2,1)S(1)}, u32[]{:S(2)}, u32[]{:S(2)}) collective-permute-start(bf16[1024,128]{1,0:T(8,128)(2,1)S(1)} %collective-permute-done.10.refs_1_), channel_id=1, source_target_pairs={{0,8},{1,9},{2,10},{3,11},{4,12},{5,13},{6,14},{7,15},{8,16},{9,17... | collective-permute-start | bytes 786440 | tf_op jit(solution)/shard_map/ppermute | solution.py:43
  44.1 22.0 %collective-permute-start.12 = (bf16[1024,128]{1,0:T(8,128)(2,1)S(1)}, bf16[1024,128]{1,0:T(8,128)(2,1)S(1)}, u32[]{:S(2)}, u32[]{:S(2)}) collective-permute-start(bf16[1024,128]{1,0:T(8,128)(2,1)S(1)} %collective-permute-done.10.refs_1_), channel_id=1, source_target_pairs={{0,24},{1,25},{2,26},{3,27},{4,28},{5,29},{6,30},{7,31},{8,0},{9,1... | collective-permute-start | bytes 786440 | tf_op jit(solution)/shard_map/ppermute | solution.py:43
  66.2 10.6 %collective-permute-start.16 = (bf16[2048,128]{1,0:T(8,128)(2,1)S(1)}, bf16[2048,128]{1,0:T(8,128)(2,1)S(1)}, u32[]{:S(2)}, u32[]{:S(2)}) collective-permute-start(bf16[2048,128]{1,0:T(8,128)(2,1)S(1)} %bitcast.19), channel_id=1, source_target_pairs={{0,8},{1,9},{2,10},{3,11},{4,12},{5,13},{6,14},{7,15},{8,16},{9,17... | collective-permute-start | bytes 1572872 | tf_op jit(solution)/shard_map/ppermute | solution.py:43
  67.3 9.6 %collective-permute-start.19 = (bf16[1024,128]{1,0:T(8,128)(2,1)S(1)}, bf16[1024,128]{1,0:T(8,128)(2,1)S(1)}, u32[]{:S(2)}, u32[]{:S(2)}) collective-permute-start(bf16[1024,128]{1,0:T(8,128)(2,1)S(1)} %collective-permute-done.9.refs_1_), channel_id=1, source_target_pairs={{0,32},{1,33},{2,34},{3,35},{4,36},{5,37},{6,38},{7,39},{8,40},{9,... | collective-permute-start | bytes 786440 | tf_op jit(solution)/shard_map/ppermute | solution.py:43
  67.3 9.6 %collective-permute-start.20 = (bf16[1024,128]{1,0:T(8,128)(2,1)S(1)}, bf16[1024,128]{1,0:T(8,128)(2,1)S(1)}, u32[]{:S(2)}, u32[]{:S(2)}) collective-permute-start(bf16[1024,128]{1,0:T(8,128)(2,1)S(1)} %collective-permute-done.11.refs_2_), channel_id=1, source_target_pairs={{0,32},{1,33},{2,34},{3,35},{4,36},{5,37},{6,38},{7,39},{8,40},{9,... | collective-permute-start | bytes 786440 | tf_op jit(solution)/shard_map/ppermute | solution.py:43
  67.8 9.1 %collective-permute-start.21 = (bf16[1024,128]{1,0:T(8,128)(2,1)S(1)}, bf16[1024,128]{1,0:T(8,128)(2,1)S(1)}, u32[]{:S(2)}, u32[]{:S(2)}) collective-permute-start(bf16[1024,128]{1,0:T(8,128)(2,1)S(1)} %collective-permute-done.12.refs_3_), channel_id=1, source_target_pairs={{0,32},{1,33},{2,34},{3,35},{4,36},{5,37},{6,38},{7,39},{8,40},{9,... | collective-permute-start | bytes 786440 | tf_op jit(solution)/shard_map/ppermute | solution.py:43
  68.5 33.5 %collective-permute-start.25 = (bf16[128,1024]{1,0:T(8,128)(2,1)S(1)}, bf16[128,1024]{1,0:T(8,128)(2,1)S(1)}, u32[]{:S(2)}, u32[]{:S(2)}) collective-permute-start(bf16[128,1024]{1,0:T(8,128)(2,1)S(1)} %copy-done.1), channel_id=1, source_target_pairs={{0,1},{1,0},{2,3},{3,2},{4,5},{5,4},{6,7},{7,6},{8,9},{9,8},{10,11... | collective-permute-start | bytes 786440 | tf_op jit(solution)/shard_map/ppermute | solution.py:43
  76.9 12.4 %collective-permute-start.17 = (bf16[2048,128]{1,0:T(8,128)(2,1)S(1)}, bf16[2048,128]{1,0:T(8,128)(2,1)S(1)}, u32[]{:S(2)}, u32[]{:S(2)}) collective-permute-start(bf16[2048,128]{1,0:T(8,128)(2,1)S(1)} %collective-permute-done.16.refs_0_), channel_id=1, source_target_pairs={{0,32},{1,33},{2,34},{3,35},{4,36},{5,37},{6,38},{7,39},{8,40},{9,... | collective-permute-start | bytes 1572872 | tf_op jit(solution)/shard_map/ppermute | solution.py:43
  92.5 7.7 %collective-permute-start.22 = (bf16[512,128]{1,0:T(8,128)(2,1)S(1)}, bf16[512,128]{1,0:T(8,128)(2,1)S(1)}, u32[]{:S(2)}, u32[]{:S(2)}) collective-permute-start(bf16[512,128]{1,0:T(8,128)(2,1)S(1)} %shard_map.57), channel_id=1, source_target_pairs={{0,64},{1,65},{2,66},{3,67},{4,68},{5,69},{6,70},{7,71},{8,72},{9,... | collective-permute-start | bytes 393224 | tf_op jit(solution)/shard_map/ppermute | solution.py:43
  100.2 7.6 %collective-permute-start.24 = (bf16[512,128]{1,0:T(8,128)(2,1)S(1)}, bf16[512,128]{1,0:T(8,128)(2,1)S(1)}, u32[]{:S(2)}, u32[]{:S(2)}) collective-permute-start(bf16[512,128]{1,0:T(8,128)(2,1)S(1)} %collective-permute-done.22.refs_1_), channel_id=1, source_target_pairs={{0,1},{1,0},{2,3},{3,2},{4,5},{5,4},{6,7},{7,6},{8,9},{9,8},{10,11... | collective-permute-start | bytes 393224 | tf_op jit(solution)/shard_map/ppermute | solution.py:43
  115.0 7.7 %collective-permute-start.28 = (bf16[1024,128]{1,0:T(8,128)(2,1)S(1)}, bf16[1024,128]{1,0:T(8,128)(2,1)S(1)}, u32[]{:S(2)}, u32[]{:S(2)}) collective-permute-start(bf16[1024,128]{1,0:T(8,128)(2,1)S(1)} %get-tuple-element.55), channel_id=1, source_target_pairs={{0,2},{1,3},{2,4},{3,5},{4,6},{5,7},{6,0},{7,1},{8,10},{9,11},{10,... | collective-permute-start | bytes 786440 | tf_op jit(solution)/shard_map/ppermute | solution.py:43
  (10 other events, 50.6 us)
